TPU v7x, 32 devices: a 4x4x1 block of a 4x4x8 slice. The times are simulated.
32 devices in a mesh: pod: 1 (over z), data: 4 (over y), expert: 8 (over x, core).
Axes of the slice: x: 4, y: 4, z: 1, core: 2. Of those that a mesh axis runs over, the one named last changes fastest.
The devices are a block of a 4x4x8 slice.
Arguments:
- tokens: bfloat16 [16384, 1536], P(('pod', 'data', 'expert'))
- routes: int32 [16384, 8], P(('pod', 'data', 'expert'))
- gates: float32 [16384, 8], P(('pod', 'data', 'expert'))
- grad_y: bfloat16 [16384, 1536], P(('pod', 'data', 'expert'))
- w_in1: bfloat16 [40, 1536, 512], P('expert')
- w_in3: bfloat16 [40, 1536, 512], P('expert')
- w_out: bfloat16 [40, 512, 1536], P('expert')
Outputs:
- output 1: bfloat16 [16384, 1536], P(('pod', 'data', 'expert'))
- output 2: bfloat16 [16384, 1536], P(('pod', 'data', 'expert'))
- output 3: float32 [40, 1536, 512], P(('pod', 'expert'))
- output 4: float32 [40, 1536, 512], P(('pod', 'expert'))
- output 5: float32 [40, 512, 1536], P(('pod', 'expert'))
All inputs are finite; a program needn't handle non-finite values.
Results may differ from a plain program's by a relative error of at most 0.0051087.
Values are sent between devices in bfloat16 or wider.
A program may use at most 768 MiB of HBM per device.

v0:
```python
import jax
import jax.numpy as jnp
from jax import lax
from jax.sharding import PartitionSpec as P

N_HOT = 2


def value_a10(tok_dev, top_k, n_exp):
    cap_hot = 3 * tok_dev // 8
    cap_cold = max(8, ((tok_dev * top_k - N_HOT * cap_hot) // (n_exp - N_HOT) + 7) // 8 * 8)
    return cap_cold, cap_hot


def route_rows(routes_dev, n_exp, cap_cold, cap_hot):
    flat_exp = routes_dev.reshape(-1)
    n_slots = flat_exp.shape[0]
    order = jnp.argsort(flat_exp, stable=True)
    counts = jax.ops.segment_sum(jnp.ones((n_slots,), jnp.int32), flat_exp, num_segments=n_exp)
    starts = jnp.cumsum(counts) - counts
    rank_sorted = jnp.arange(n_slots, dtype=jnp.int32) - starts[flat_exp[order]]
    slot_rank = jnp.zeros((n_slots,), jnp.int32).at[order].set(rank_sorted)
    hot_index = jnp.where(flat_exp == 0, 0, jnp.where(flat_exp == n_exp // 2, 1, -1))
    cold_row = jnp.where((hot_index < 0) & (slot_rank < cap_cold), flat_exp * cap_cold + slot_rank, n_exp * cap_cold)
    hot_row = jnp.where(hot_index >= 0, hot_index * cap_hot + slot_rank, N_HOT * cap_hot)
    return cold_row, hot_row


def gather_rows(slot_rows, x_local, dy_local, gate_flat, n_rows):
    n_slots = slot_rows.shape[0]
    tok_n = x_local.shape[0]
    top_k = n_slots // tok_n
    src_tok = jnp.full((n_rows,), tok_n, jnp.int32).at[slot_rows].set(
        jnp.arange(n_slots, dtype=jnp.int32) // top_k, mode='drop')
    src_gate = jnp.zeros((n_rows,), jnp.float32).at[slot_rows].set(gate_flat, mode='drop')
    x_rows = jnp.take(x_local, src_tok, axis=0, mode='fill', fill_value=0)
    dy_rows = jnp.take(dy_local, src_tok, axis=0, mode='fill', fill_value=0)
    do_rows = (dy_rows.astype(jnp.float32) * src_gate[:, None]).astype(jnp.bfloat16)
    return x_rows, do_rows


def expert_fwd(x_rows, w_a, w_b, w_c):
    pre_a = jnp.einsum('esd,edf->esf', x_rows, w_a, preferred_element_type=jnp.float32).astype(jnp.bfloat16)
    pre_b = jnp.einsum('esd,edf->esf', x_rows, w_b, preferred_element_type=jnp.float32).astype(jnp.bfloat16)
    act_a = pre_a.astype(jnp.float32)
    hidden = (act_a * jax.nn.sigmoid(act_a) * pre_b.astype(jnp.float32)).astype(jnp.bfloat16)
    outs = jnp.einsum('esf,efd->esd', hidden, w_c, preferred_element_type=jnp.float32).astype(jnp.bfloat16)
    return outs, pre_a, pre_b, hidden


def expert_bwd(x_rows, do_rows, pre_a, pre_b, hidden, w_a, w_b, w_c):
    d_hidden = jnp.einsum('esd,efd->esf', do_rows, w_c, preferred_element_type=jnp.float32)
    act_a = pre_a.astype(jnp.float32)
    act_b = pre_b.astype(jnp.float32)
    sigma_a = jax.nn.sigmoid(act_a)
    d_pre_b = (d_hidden * act_a * sigma_a).astype(jnp.bfloat16)
    d_pre_a = (d_hidden * act_b * sigma_a * (1.0 + act_a * (1.0 - sigma_a))).astype(jnp.bfloat16)
    d_rows = (jnp.einsum('esf,edf->esd', d_pre_a, w_a, preferred_element_type=jnp.float32)
              + jnp.einsum('esf,edf->esd', d_pre_b, w_b, preferred_element_type=jnp.float32)).astype(jnp.bfloat16)
    grad_a = jnp.einsum('esd,esf->edf', x_rows, d_pre_a, preferred_element_type=jnp.float32)
    grad_b = jnp.einsum('esd,esf->edf', x_rows, d_pre_b, preferred_element_type=jnp.float32)
    grad_c = jnp.einsum('esf,esd->efd', hidden, do_rows, preferred_element_type=jnp.float32)
    return d_rows, grad_a, grad_b, grad_c


def combine(cold_rows, hot_rows, cold_vals, hot_vals, weights, tok_n):
    slot_vals = (jnp.take(cold_vals, cold_rows, axis=0, mode='fill', fill_value=0)
                 + jnp.take(hot_vals, hot_rows, axis=0, mode='fill', fill_value=0))
    slot_vals = slot_vals.reshape(tok_n, -1, cold_vals.shape[1]).astype(jnp.float32)
    if weights is not None:
        slot_vals = slot_vals * weights[:, :, None]
    return jnp.sum(slot_vals, axis=1).astype(jnp.bfloat16)


def solution(mesh):
    n_dev = mesh.shape['expert']
    row_spec = P(('pod', 'data', 'expert'), None)
    w_spec = P('expert', None, None)
    grad_spec = P(('pod', 'expert'), None, None)

    def body(tokens, routes, gates, grad_y, w_in1, w_in3, w_out):
        tok_n, d_model = tokens.shape
        top_k = routes.shape[1]
        exp_local = w_in1.shape[0]
        n_exp = exp_local * n_dev
        my_index = lax.axis_index('expert')
        cap_cold, cap_hot = value_a10(tok_n, top_k, n_exp)
        cold_rows, hot_rows = route_rows(routes, n_exp, cap_cold, cap_hot)
        gate_flat = gates.reshape(-1)
        cold_x, cold_do = gather_rows(cold_rows, tokens, grad_y, gate_flat, n_exp * cap_cold)
        hot_x, hot_do = gather_rows(hot_rows, tokens, grad_y, gate_flat, N_HOT * cap_hot)
        hot_x = hot_x.reshape(N_HOT, cap_hot, d_model)
        hot_do = hot_do.reshape(N_HOT, cap_hot, d_model)
        hot_local = [0, (n_exp // 2) % exp_local]
        hot_owner = [0, (n_exp // 2) // exp_local]

        def owned_copy(w_local):
            return jnp.stack([jnp.where(my_index == owner_idx, w_local[local_idx], 0)
                              for local_idx, owner_idx in zip(hot_local, hot_owner)])

        hot_w1, hot_w3, hot_w2 = lax.psum((owned_copy(w_in1), owned_copy(w_in3), owned_copy(w_out)), 'expert')

        recv_x = lax.all_to_all(cold_x.reshape(n_exp, cap_cold, d_model), 'expert', 0, 1, tiled=True)
        cold_out, cold_pre_a, cold_pre_b, cold_hidden = expert_fwd(recv_x, w_in1, w_in3, w_out)
        back_out = lax.all_to_all(cold_out, 'expert', 1, 0, tiled=True)
        hot_out, hot_pre_a, hot_pre_b, hot_hidden = expert_fwd(hot_x, hot_w1, hot_w3, hot_w2)
        y_out = combine(cold_rows, hot_rows, back_out.reshape(-1, d_model), hot_out.reshape(-1, d_model), gates, tok_n)

        recv_do = lax.all_to_all(cold_do.reshape(n_exp, cap_cold, d_model), 'expert', 0, 1, tiled=True)
        cold_dx, grad_w1, grad_w3, grad_w2 = expert_bwd(recv_x, recv_do, cold_pre_a, cold_pre_b, cold_hidden, w_in1, w_in3, w_out)
        back_dx = lax.all_to_all(cold_dx, 'expert', 1, 0, tiled=True)
        hot_dx, part_w1, part_w3, part_w2 = expert_bwd(hot_x, hot_do, hot_pre_a, hot_pre_b, hot_hidden, hot_w1, hot_w3, hot_w2)
        grad_x = combine(cold_rows, hot_rows, back_dx.reshape(-1, d_model), hot_dx.reshape(-1, d_model), None, tok_n)
        part_w1, part_w3, part_w2 = lax.psum((part_w1, part_w3, part_w2), 'expert')

        def add_owned(grad_local, hot_sum):
            for slot_h in range(N_HOT):
                grad_local = grad_local.at[hot_local[slot_h]].add(
                    jnp.where(my_index == hot_owner[slot_h], hot_sum[slot_h], 0.0))
            return grad_local

        grad_w1 = add_owned(grad_w1, part_w1)
        grad_w3 = add_owned(grad_w3, part_w3)
        grad_w2 = add_owned(grad_w2, part_w2)
        grad_w1, grad_w3, grad_w2 = lax.psum((grad_w1, grad_w3, grad_w2), 'data')
        return y_out, grad_x, grad_w1, grad_w3, grad_w2

    return jax.shard_map(body, mesh=mesh,
                         in_specs=(row_spec, row_spec, row_spec, row_spec, w_spec, w_spec, w_spec),
                         out_specs=(row_spec, row_spec, grad_spec, grad_spec, grad_spec),
                         check_vma=False)
```

profile of v0, /device:TPU:97, one launch (start us, length us, event | category | flops | bytes accessed | tf_op | source)
XLA Modules:
  0.0 1608.7 jit_solution(16060491352789923766)
XLA Ops:
  8.3 28.8 %scatter_custom_fusion = s32[40]{0:T(128)S(1)} fusion(s32[4096]{0:T(1024)S(1)} %reshape.276, s32[4096]{0:T(1024)S(1)} %broadcast_in_dim.111, s32[]{:T(128)} %constant.213.clone.1), kind=kCustom, calls=%fused_computation.169 | custom fusion | flops 4096 | bytes 164 | tf_op jit(solution)/shard_map/scatter-add | solution.py:19
  39.5 5.8 sort.17
  45.3 23.0 %gather_fusion = s32[4096]{0:T(1024)S(1)} fusion(s32[4096]{0:T(1024)S(1)} %reshape.276, s32[4096]{0:T(1024)S(1)} %get-tuple-element.139), kind=kCustom, calls=%fused_computation.8 | custom fusion | bytes 49152 | tf_op jit(solution)/shard_map/gather | solution.py:21
  68.3 4.4 compare_select_fusion.1
  74.4 20.9 %select_subtract_fusion = s32[4096]{0:T(1024)S(1)} fusion(pred[4096]{0:T(1024)(128)(4,1)S(1)} %get-tuple-element.115, pred[4096]{0:T(1024)(128)(4,1)S(1)} %get-tuple-element.114, pred[4096]{0:T(1024)(128)(4,1)S(1)} %get-tuple-element.113, pred[4096]{0:T(1024)(128)(4,1)S(1)} %get-tuple-element.112, pred[4096]{0:T(1024)(128)(4,1)S(1)} %get-tuple-element.111, ...), kind=kLoop, calls=%fused_computation.143 | loop fusion | flops 139264 | bytes 168068 | tf_op jit(solution)/shard_map/sub | solution.py:21
  95.3 15.5 scatter_custom_fusion.1
  111.4 15.5 scatter_custom_fusion.2
  127.0 15.0 gather_fusion.1
  142.0 11.3 broadcast_select_fusion
  153.3 7.8 all-to-all-start
  161.4 15.0 gather_fusion.5
  176.4 15.5 scatter_custom_fusion.4
  195.5 4.0 broadcast_select_fusion.5
  199.5 3.7 broadcast_select_fusion.6
  203.3 6.8 multiply_convert_fusion
  210.0 91.6 %all-to-all-done = bf16[40,104,1536]{2,1,0:T(8,128)(2,1)} async-done(((bf16[40,104,1536]{2,1,0:T(8,128)(2,1)}), bf16[40,104,1536]{2,1,0:T(8,128)(2,1)}, u32[]{:S(2)}, u32[]{:S(2)}) %all-to-all-start) | async-done | bytes 12779552 | tf_op jit(solution)/shard_map/all_to_all | solution.py:103
  301.6 6.3 all-to-all-start.2
  308.0 4.0 pad_maximum_fusion.1
  314.1 15.5 scatter_custom_fusion.3
  335.2 15.7 scatter_custom_fusion.5
  354.0 182.3 %all-reduce.11.cloned.1.call-done = (bf16[2,512,1536]{2,1,0:T(8,128)(2,1)}, bf16[2,1536,512]{2,1,0:T(8,128)(2,1)}, bf16[2,1536,512]{2,1,0:T(8,128)(2,1)}) async-done(((bf16[2,512,1536]{2,1,0:T(8,128)(2,1)}, bf16[2,1536,512]{2,1,0:T(8,128)(2,1)}, bf16[2,1536,512]{2,1,0:T(8,128)(2,1)}), (bf16[2,512,1536]{2,1,0:T(8,128)(2,1)}, bf16[2,1536,512]{2,1,0:T(8,128)(2,1)}, ...) | async-done | bytes 9437200 | tf_op jit(solution)/shard_map/psum | solution.py:101
  539.2 3.3 fusion.69
  543.6 3.7 fusion.72
  547.3 3.8 fusion.53
  551.1 3.7 fusion.56
  555.4 6.6 copy.26
  562.0 16.3 %convolution_convert_fusion.2 = bf16[5,832,512]{2,1,0:T(8,128)(2,1)} fusion(bf16[5,832,1536]{2,1,0:T(8,128)(2,1)S(1)} %bitcast.112, bf16[5,1536,512]{2,1,0:T(8,128)(2,1)} %param.32), kind=kOutput, calls=%fused_computation.61 | convolution fusion | flops 6545244160 | bytes 24903680 | tf_op jit(solution)/shard_map/esd,edf->esf/dot_general | solution.py:44
  578.3 8.3 convolution_convert_fusion.3
  586.6 10.9 copy.31
  597.5 17.7 %fusion.4 = (bf16[5,832,512]{2,1,0:T(8,128)(2,1)}, f32[5,832,512]{2,1,0:T(8,128)}) fusion(bf16[5,832,512]{2,1,0:T(8,128)(2,1)} %convolution_convert_fusion.2, bf16[5,832,512]{2,1,0:T(8,128)(2,1)} %convolution_convert_fusion.3, bf16[5,832,1536]{2,1,0:T(8,128)(2,1)} %bitcast.116, bf16[5,512,1536]{2,1,0:T(8,128)(2,1)} %param.33), kind=kOutput, calls=%fused_computation.33 | convolution fusion | flops 6568673280 | bytes 41943040 | tf_op jit(solution)/shard_map/esd,efd->esf/dot_general | solution.py:52
  615.2 18.8 %fusion.62 = f32[5,1536,512]{2,1,0:T(8,128)} fusion(bf16[5,832,1536]{2,1,0:T(8,128)(2,1)} %bitcast.114, f32[5,832,512]{2,1,0:T(8,128)} %get-tuple-element.184, bf16[5,832,512]{2,1,0:T(8,128)(2,1)} %convolution_convert_fusion.3), kind=kOutput, calls=%fused_computation.174 | convolution fusion | flops 6558023680 | bytes 41287680 | tf_op jit(solution)/shard_map/esd,esf->edf/dot_general | solution.py:61
  634.0 14.5 copy.40
  648.5 16.2 %fusion.71 = f32[5,1536,512]{2,1,0:T(8,128)} fusion(bf16[5,832,1536]{2,1,0:T(8,128)(2,1)} %bitcast.115, bf16[5,832,512]{2,1,0:T(8,128)(2,1)} %get-tuple-element.183), kind=kOutput, calls=%fused_computation.181 | convolution fusion | flops 6543114240 | bytes 32768000 | tf_op jit(solution)/shard_map/esd,esf->edf/dot_general | solution.py:60
  664.7 14.2 copy.41
  678.9 18.0 %fusion.59 = f32[5,512,1536]{2,1,0:T(8,128)} fusion(bf16[5,832,1536]{2,1,0:T(8,128)(2,1)} %bitcast.117, bf16[5,832,512]{2,1,0:T(8,128)(2,1)} %convolution_convert_fusion.2, bf16[5,832,512]{2,1,0:T(8,128)(2,1)} %convolution_convert_fusion.3), kind=kOutput, calls=%fused_computation.173 | convolution fusion | flops 6560153600 | bytes 37027840 | tf_op jit(solution)/shard_map/esf,esd->efd/dot_general | solution.py:62
  696.9 13.8 copy.44
  710.7 42.5 %all-reduce.7.cloned.1.call-done = (f32[2,1536,512]{2,1,0:T(8,128)}, f32[2,1536,512]{2,1,0:T(8,128)}, f32[2,512,1536]{2,1,0:T(8,128)}) async-done(((f32[2,1536,512]{2,1,0:T(8,128)}, f32[2,1536,512]{2,1,0:T(8,128)}, f32[2,512,1536]{2,1,0:T(8,128)}), (f32[2,1536,512]{2,1,0:T(8,128)}, f32[2,1536,512]{2,1,0:T(8,128)}, f32[2,512,1536]{2,1,0:T(8,128)})) %all-reduce.7.cloned.1.call-update) | async-done | bytes 18874384 | tf_op jit(solution)/shard_map/psum | solution.py:114
  753.2 5.4 fusion.24
  758.6 5.7 fusion.12
  764.3 4.3 fusion.23
  768.6 4.3 fusion.22
  773.0 6.3 fusion.15
  779.3 14.5 convolution_convert_fusion
  793.8 31.8 %copy.27 = bf16[5,832,1536]{2,0,1:T(8,128)(2,1)} copy(bf16[5,832,1536]{2,1,0:T(8,128)(2,1)} %convolution_convert_fusion) | data formatting | bytes 25559040 | tf_op jit(solution)/shard_map/convert_element_type | solution.py:47
  825.6 7.2 all-to-all-start.1
  832.9 15.4 fusion.68
  848.3 21.8 %add_convert_fusion = bf16[5,832,1536]{2,1,0:T(8,128)(2,1)} fusion(f32[5,832,1536]{2,1,0:T(8,128)} %fusion.68, bf16[5,1536,512]{2,1,0:T(8,128)(2,1)} %param.32, f32[5,832,512]{2,1,0:T(8,128)} %get-tuple-element.184, bf16[5,832,512]{2,1,0:T(8,128)(2,1)} %convolution_convert_fusion.3), kind=kOutput, calls=%fused_computation.15 | convolution fusion | flops 6570803200 | bytes 58982400 | tf_op jit(solution)/shard_map/esf,edf->esd/dot_general | solution.py:59
  870.1 31.7 %copy.32 = bf16[5,832,1536]{2,0,1:T(8,128)(2,1)} copy(bf16[5,832,1536]{2,1,0:T(8,128)(2,1)} %add_convert_fusion) | data formatting | bytes 25559040 | tf_op jit(solution)/shard_map/convert_element_type | solution.py:59
  901.9 153.7 %all-to-all-done.1 = bf16[5,832,1536]{2,0,1:T(8,128)(2,1)} async-done(((bf16[5,832,1536]{2,0,1:T(8,128)(2,1)}), bf16[5,832,1536]{2,0,1:T(8,128)(2,1)}, u32[]{:S(2)}, u32[]{:S(2)}) %all-to-all-start.1) | async-done | bytes 12779552 | tf_op jit(solution)/shard_map/all_to_all | solution.py:105
  1055.5 7.4 all-to-all-start.3
  1065.7 19.3 %gather_fusion.4 = bf16[4096,1536]{1,0:T(8,128)(2,1)} fusion(bf16[384,1536]{1,0:T(8,128)(2,1)S(1)} %bitcast.99, s32[4096]{0:T(1024)S(1)} %get-tuple-element.187), kind=kCustom, calls=%fused_computation.3.clone | custom fusion | bytes 25182208 | tf_op jit(solution)/shard_map/jit(_take)/gather | solution.py:68
  1088.0 3.1 fusion.20
  1091.1 19.3 %gather_fusion.8 = bf16[4096,1536]{1,0:T(8,128)(2,1)} fusion(bf16[384,1536]{1,0:T(8,128)(2,1)S(1)} %bitcast.98, s32[4096]{0:T(1024)S(1)} %get-tuple-element.187), kind=kCustom, calls=%fused_computation.7.clone | custom fusion | bytes 25182208 | tf_op jit(solution)/shard_map/jit(_take)/gather | solution.py:68
  1110.4 15.6 copy.28
  1126.0 159.6 %all-to-all-done.3 = bf16[5,832,1536]{2,0,1:T(8,128)(2,1)} async-done(((bf16[5,832,1536]{2,0,1:T(8,128)(2,1)}), bf16[5,832,1536]{2,0,1:T(8,128)(2,1)}, u32[]{:S(2)}, u32[]{:S(2)}) %all-to-all-start.3) | async-done | bytes 12779552 | tf_op jit(solution)/shard_map/all_to_all | solution.py:111
  1285.6 15.6 copy.33
  1301.2 31.6 %gather_fusion.2 = bf16[4096,1536]{1,0:T(8,128)(2,1)} fusion(bf16[4160,1536]{1,0:T(8,128)(2,1)} %bitcast.100, s32[4096]{0:T(1024)S(1)} %get-tuple-element.188), kind=kCustom, calls=%fused_computation.1.clone | custom fusion | bytes 25182208 | tf_op jit(solution)/shard_map/jit(_take)/gather | solution.py:67
  1332.8 31.5 %gather_fusion.6 = bf16[4096,1536]{1,0:T(8,128)(2,1)} fusion(bf16[4160,1536]{1,0:T(8,128)(2,1)} %bitcast.101, s32[4096]{0:T(1024)S(1)} %get-tuple-element.188), kind=kCustom, calls=%fused_computation.5.clone | custom fusion | bytes 25182208 | tf_op jit(solution)/shard_map/jit(_take)/gather | solution.py:67
  1364.4 17.0 %bitcast_reduce_fusion = bf16[512,1536]{1,0:T(8,128)(2,1)} fusion(bf16[4096,1536]{1,0:T(8,128)(2,1)} %gather_fusion.8, bf16[4096,1536]{1,0:T(8,128)(2,1)} %gather_fusion.6, pred[4096]{0:T(1024)(128)(4,1)S(1)} %copy-done.26, pred[4096]{0:T(1024)(128)(4,1)S(1)} %copy-done.25), kind=kLoop, calls=%fused_computation.24 | loop fusion | flops 24379392 | bytes 26746880 | tf_op jit(solution)/shard_map/reduce_sum | solution.py:72
  1381.3 16.3 %fusion = bf16[512,1536]{1,0:T(8,128)(2,1)} fusion(bf16[4096,1536]{1,0:T(8,128)(2,1)} %gather_fusion.4, bf16[4096,1536]{1,0:T(8,128)(2,1)S(1)} %copy-done.4, f32[512,8]{1,0:T(8,128)S(1)} %copy-done.16, pred[4096]{0:T(1024)(128)(4,1)S(1)} %copy-done.26, pred[4096]{0:T(1024)(128)(4,1)S(1)} %copy-done.25), kind=kLoop, calls=%fused_computation.18 | loop fusion | flops 55836672 | bytes 26763264 | tf_op jit(solution)/shard_map/reduce_sum | solution.py:72
  1397.6 160.8 %all-reduce.9.cloned.1.call-done = (f32[5,1536,512]{2,1,0:T(8,128)}, f32[5,1536,512]{2,1,0:T(8,128)}, f32[5,512,1536]{2,1,0:T(8,128)}) async-done(((f32[5,1536,512]{2,1,0:T(8,128)}, f32[5,1536,512]{2,1,0:T(8,128)}, f32[5,512,1536]{2,1,0:T(8,128)}), (f32[5,1536,512]{2,1,0:T(8,128)}, f32[5,1536,512]{2,1,0:T(8,128)}, f32[5,512,1536]{2,1,0:T(8,128)})) %all-reduce.9.cloned.1.call-update) | async-done | bytes 47185936 | tf_op jit(solution)/shard_map/psum | solution.py:125
  1558.5 14.5 copy.49
  1573.0 14.5 copy.50
  1587.6 14.2 copy.51
  (108 shorter events, 30.7 us)
Async XLA Ops:
  7.2 119.9 %copy-start = (bf16[512,1536]{1,0:T(8,128)(2,1)S(1)}, bf16[512,1536]{1,0:T(8,128)(2,1)}, u32[]{:S(2)}) copy-start(bf16[512,1536]{1,0:T(8,128)(2,1)} %param.27) | copy-start | bytes 4718596
  111.4 65.0 %copy-start.21 = (s32[4096]{0:T(1024)}, s32[4096]{0:T(1024)S(1)}, u32[]{:S(2)}) copy-start(s32[4096]{0:T(1024)S(1)} %get-tuple-element.126) | copy-start | bytes 49156
  111.4 223.8 %copy-start.23 = (s32[4096]{0:T(1024)}, s32[4096]{0:T(1024)S(1)}, u32[]{:S(2)}) copy-start(s32[4096]{0:T(1024)S(1)} %get-tuple-element.138) | copy-start | bytes 49156
  153.3 7.8 copy-start.27
  153.3 8.1 copy-start.2
  153.3 148.3 %all-to-all-start = ((bf16[40,104,1536]{2,1,0:T(8,128)(2,1)}), bf16[40,104,1536]{2,1,0:T(8,128)(2,1)}, u32[]{:S(2)}, u32[]{:S(2)}) async-start(bf16[40,104,1536]{2,1,0:T(8,128)(2,1)} %bitcast.103), calls=%async_computation | async-start | bytes 25559040 | tf_op jit(solution)/shard_map/all_to_all | solution.py:103
  161.2 15.2 copy-start.15
  193.6 9.7 copy-start.3
  301.6 285.0 %all-to-all-start.2 = ((bf16[40,104,1536]{2,1,0:T(8,128)(2,1)}), bf16[40,104,1536]{2,1,0:T(8,128)(2,1)}, u32[]{:S(2)}, u32[]{:S(2)}) async-start(bf16[40,104,1536]{2,1,0:T(8,128)(2,1)} %bitcast.102), calls=%async_computation.2 | async-start | bytes 25559040 | tf_op jit(solution)/shard_map/all_to_all | solution.py:109
  307.9 228.4 %all-reduce.11.cloned.1.call-start = ((), (), s32[]{:S(2)}) async-start(), calls=%async_computation.6 | async-start | bytes 18874368 | tf_op jit(solution)/shard_map/psum | solution.py:101
  308.0 4.0 copy-start.8
  308.0 4.0 copy-start.9
  314.0 439.2 %all-reduce.7.cloned.1.call-start = ((), (), s32[]{:S(2)}) async-start(), calls=%async_computation.4 | async-start | bytes 37748736 | tf_op jit(solution)/shard_map/psum | solution.py:114
  536.4 6.2 copy-start.14
  539.2 11.9 copy-start.12
  542.5 4.8 copy-start.10
  543.6 7.5 copy-start.17
  543.6 7.5 copy-start.19
  554.8 1003.6 %all-reduce.9.cloned.1.call-start = ((), (), s32[]{:S(2)}) async-start(), calls=%async_computation.5 | async-start | bytes 94371840 | tf_op jit(solution)/shard_map/psum | solution.py:125
  555.4 22.9 %slice-start = ((s8[7864320]{0:T(1024)(128)(4,1)}), s8[4194304]{0:T(1024)(128)(4,1)S(1)}, s32[]{:S(2)}) async-start(s8[7864320]{0:T(1024)(128)(4,1)} %bitcast.108), calls=%async_computation.7 | async-start | bytes 8388608
  562.0 16.3 %copy-start.7 = (bf16[5,8,104,1536]{3,2,1,0:T(8,128)(2,1)}, bf16[5,8,104,1536]{3,2,1,0:T(8,128)(2,1)S(1)}, u32[]{:S(2)}) copy-start(bf16[5,8,104,1536]{3,2,1,0:T(8,128)(2,1)S(1)} %copy.26) | copy-start | bytes 38338564
  562.0 16.3 %slice-start.1 = ((s8[7864320]{0:T(1024)(128)(4,1)}), s8[3670016]{0:T(1024)(128)(4,1)S(1)}, s32[]{:S(2)}) async-start(s8[7864320]{0:T(1024)(128)(4,1)} %bitcast.108), calls=%async_computation.8 | async-start | bytes 7340032
  753.2 5.4 copy-start.5
  753.2 15.4 slice-start.2
  758.6 5.8 copy-start.6
  758.6 10.1 slice-start.3
  825.6 229.9 %all-to-all-start.1 = ((bf16[5,832,1536]{2,0,1:T(8,128)(2,1)}), bf16[5,832,1536]{2,0,1:T(8,128)(2,1)}, u32[]{:S(2)}, u32[]{:S(2)}) async-start(bf16[5,832,1536]{2,0,1:T(8,128)(2,1)} %copy.27), calls=%async_computation.1 | async-start | bytes 40894464 | tf_op jit(solution)/shard_map/all_to_all | solution.py:105
  901.8 161.1 %copy-start.22 = (s32[4096]{0:T(1024)S(1)}, s32[4096]{0:T(1024)}, u32[]{:S(2)}) copy-start(s32[4096]{0:T(1024)} %copy-done.21) | copy-start | bytes 49156
  901.8 161.1 %copy-start.24 = (s32[4096]{0:T(1024)S(1)}, s32[4096]{0:T(1024)}, u32[]{:S(2)}) copy-start(s32[4096]{0:T(1024)} %copy-done.23) | copy-start | bytes 49156
  901.8 161.1 %copy-start.13 = (f32[2,192,512]{2,1,0:T(8,128)S(1)}, f32[2,192,512]{2,1,0:T(8,128)}, u32[]{:S(2)}) copy-start(f32[2,192,512]{2,1,0:T(8,128)} %copy-done.12) | copy-start | bytes 2359300
  901.8 161.1 %copy-start.18 = (bf16[2,192,512]{2,1,0:T(8,128)(2,1)S(1)}, bf16[2,192,512]{2,1,0:T(8,128)(2,1)}, u32[]{:S(2)}) copy-start(bf16[2,192,512]{2,1,0:T(8,128)(2,1)} %copy-done.17) | copy-start | bytes 1179652
  1055.5 230.1 %all-to-all-start.3 = ((bf16[5,832,1536]{2,0,1:T(8,128)(2,1)}), bf16[5,832,1536]{2,0,1:T(8,128)(2,1)}, u32[]{:S(2)}, u32[]{:S(2)}) async-start(bf16[5,832,1536]{2,0,1:T(8,128)(2,1)} %copy.32), calls=%async_computation.3 | async-start | bytes 40894464 | tf_op jit(solution)/shard_map/all_to_all | solution.py:111
  1065.7 19.3 %copy-start.20 = (bf16[2,192,512]{2,1,0:T(8,128)(2,1)S(1)}, bf16[2,192,512]{2,1,0:T(8,128)(2,1)}, u32[]{:S(2)}) copy-start(bf16[2,192,512]{2,1,0:T(8,128)(2,1)} %copy-done.19) | copy-start | bytes 1179652
  1065.7 22.3 %copy-start.11 = (f32[2,192,512]{2,1,0:T(8,128)S(1)}, f32[2,192,512]{2,1,0:T(8,128)}, u32[]{:S(2)}) copy-start(f32[2,192,512]{2,1,0:T(8,128)} %copy-done.10) | copy-start | bytes 2359300
  1332.8 31.5 %copy-start.25 = (pred[4096]{0:T(1024)(128)(4,1)S(1)}, pred[4096]{0:T(1024)(128)(4,1)}, u32[]{:S(2)}) copy-start(pred[4096]{0:T(1024)(128)(4,1)} %get-tuple-element.125) | copy-start | bytes 12292
  1332.8 31.5 %copy-start.26 = (pred[4096]{0:T(1024)(128)(4,1)S(1)}, pred[4096]{0:T(1024)(128)(4,1)}, u32[]{:S(2)}) copy-start(pred[4096]{0:T(1024)(128)(4,1)} %get-tuple-element.137) | copy-start | bytes 12292
  1364.4 17.0 %copy-start.4 = (bf16[4096,1536]{1,0:T(8,128)(2,1)S(1)}, bf16[4096,1536]{1,0:T(8,128)(2,1)}, u32[]{:S(2)}) copy-start(bf16[4096,1536]{1,0:T(8,128)(2,1)} %gather_fusion.2) | copy-start | bytes 37748740
  1364.4 17.0 %copy-start.16 = (f32[512,8]{1,0:T(8,128)S(1)}, f32[512,8]{1,0:T(8,128)}, u32[]{:S(2)}) copy-start(f32[512,8]{1,0:T(8,128)} %copy-done.15) | copy-start | bytes 49156
  1587.6 14.2 copy-start.1
Sparse Core Ops, SparseCore 0:
  314.1 222.2 all-reduce.10
  555.0 198.1 all-reduce.6
  779.4 779.0 all-reduce.8
where the time goes:
time: 1620 us; the launch traced here: 1610 us
  waiting for transfers between devices  791 us (49%)
  local copies, waits for them, and re-layouts  440 us (27%)
  matrix products  174 us (11%)
  other arithmetic  160 us (10%)
  starting transfers between devices  29.3 us (2%)
    psum x1, waiting for transfers between devices, body(): lax.psum((owned_copy(w_in1), owned_copy(w_in3), owned_copy(w_out)), 'expe...  182 us
    psum x1, waiting for transfers between devices, body(): grad_w1, grad_w3, grad_w2 = lax.psum((grad_w1, grad_w3, grad_w2), 'data')  161 us
    all_to_all x1, waiting for transfers between devices, body(): back_dx = lax.all_to_all(cold_dx, 'expert', 1, 0, tiled=True)  160 us
    all_to_all x1, waiting for transfers between devices, body(): back_out = lax.all_to_all(cold_out, 'expert', 1, 0, tiled=True)  154 us
    all_to_all x1, waiting for transfers between devices, body(): lax.all_to_all(cold_x.reshape(n_exp, cap_cold, d_model), 'expert', 0, 1,...  91.6 us
    unnamed x72, local copies, waits for them, and re-layouts  87.1 us
    gather x2, local copies, waits for them, and re-layouts, combine(): jnp.take(cold_vals, cold_rows, axis=0, mode='fill', fill_value=0)  63.1 us
    psum x1, waiting for transfers between devices, body(): part_w1, part_w3, part_w2 = lax.psum((part_w1, part_w3, part_w2), 'expert')  42.5 us
  transfers between devices with their start and end apart: 7, of which 6 were waited for; matrix products, arithmetic and copies ran while one was open for 35% of the time, Pallas kernels for 0%

commit v1 on v0

v1 whole, which is shorter than its diff:
```python
import functools

import jax
import jax.numpy as jnp
from jax import lax
from jax.experimental import pallas as pl
from jax.experimental.pallas import tpu as pltpu
from jax.sharding import PartitionSpec as P

N_HOT = 2
BF = jnp.bfloat16
F32 = jnp.float32
VMEM_LIMIT = 60 * 1024 * 1024


def value_a10(tok_dev, top_k, n_exp):
    cap_hot = 3 * tok_dev // 8
    cap_cold = max(8, ((tok_dev * top_k - N_HOT * cap_hot) // (n_exp - N_HOT) + 7) // 8 * 8)
    return cap_cold, cap_hot


def dot(a, b, ca=1, cb=0):
    return lax.dot_general(a, b, (((ca,), (cb,)), ((), ())), preferred_element_type=F32)


def params(n_axes):
    return pltpu.CompilerParams(dimension_semantics=("arbitrary",) * n_axes, vmem_limit_bytes=VMEM_LIMIT)


def cost(flops, nbytes):
    return pl.CostEstimate(flops=int(flops), bytes_accessed=int(nbytes), transcendentals=0)


def gather_body(caps, gated, rank_ref, *refs):
    if gated:
        gate_ref, src_ref, hot_ref, cold_ref = refs
    else:
        src_ref, hot_ref, cold_ref = refs
    tok_n = src_ref.shape[1]
    picks, scales = [], []
    for i, cap in enumerate(caps):
        hit = lax.broadcasted_iota(jnp.int32, (cap, tok_n), 0) == rank_ref[0, i:i + 1, :]
        picks.append(jnp.where(hit, 1.0, 0.0))
        if gated:
            scales.append(jnp.sum(jnp.where(hit, gate_ref[0, i:i + 1, :], 0.0), axis=1, keepdims=True))
    pick = jnp.concatenate(picks, axis=0).astype(BF)
    width = 256
    for n in range(src_ref.shape[2] // width):
        cols = pl.ds(n * width, width)
        rows = dot(pick, src_ref[0, :, cols])
        start = 0
        for i, cap in enumerate(caps):
            part = rows[start:start + cap]
            if gated:
                part = part * scales[i]
            part = part.astype(BF)
            if i == 0:
                hot_ref[0, :, cols] = part
            else:
                cold_ref[i - 1, 0, :, cols] = part
            start += cap


def gather_rows(caps, rank, gate, src):
    n_src, tok_n, d = src.shape
    n_loc = len(caps)
    table = pl.BlockSpec((1, n_loc, tok_n), lambda s: (s, 0, 0))
    ins = [rank] + ([gate] if gate is not None else []) + [src]
    return pl.pallas_call(
        functools.partial(gather_body, caps, gate is not None),
        grid=(n_src,),
        in_specs=[table] * (len(ins) - 1) + [pl.BlockSpec((1, tok_n, d), lambda s: (s, 0, 0))],
        out_specs=[pl.BlockSpec((1, caps[0], d), lambda s: (s, 0, 0)),
                   pl.BlockSpec((n_loc - 1, 1, caps[1], d), lambda s: (0, s, 0, 0))],
        out_shape=[jax.ShapeDtypeStruct((n_src, caps[0], d), BF),
                   jax.ShapeDtypeStruct((n_loc - 1, n_src, caps[1], d), BF)],
        compiler_params=params(1),
        cost_estimate=cost(2 * n_src * sum(caps) * tok_n * d, 2 * n_src * d * (tok_n + sum(caps))),
        name="gather_do" if gate is not None else "gather_x",
    )(*ins)


def fwd_body(x_ref, w1_ref, w3_ref, a_ref, b_ref):
    x = x_ref[0]
    a_ref[0] = dot(x, w1_ref[0]).astype(BF)
    b_ref[0] = dot(x, w3_ref[0]).astype(BF)


def expert_in(x_rows, w1, w3, m, off):
    n_e, n_r, d = x_rows.shape
    f = w1.shape[2]
    row = lambda width: pl.BlockSpec((1, m, width), lambda e, c: (e, c, 0))
    wsp = pl.BlockSpec((1, d, f), lambda e, c: (e + off, 0, 0))
    return pl.pallas_call(
        fwd_body, grid=(n_e, n_r // m), in_specs=[row(d), wsp, wsp], out_specs=[row(f), row(f)],
        out_shape=[jax.ShapeDtypeStruct((n_e, n_r, f), BF)] * 2, compiler_params=params(2),
        cost_estimate=cost(4 * n_e * n_r * d * f, 2 * n_e * n_r * (d + 2 * f)), name="expert_in",
    )(x_rows, w1, w3)


def hidden_of(a_ref, b_ref):
    a = a_ref[0].astype(F32)
    return (a * jax.nn.sigmoid(a) * b_ref[0].astype(F32)).astype(BF)


def out_body(q_ref, a_ref, b_ref, w2_ref, o_ref):
    o_ref[0] = dot(hidden_of(a_ref, b_ref), w2_ref[0]).astype(BF)


def own_out(q, a, b, w2, m, n_own, off):
    n_e, _, f = a.shape
    d = w2.shape[2]
    row = pl.BlockSpec((1, m, f), lambda e, c, q_ref: (e, q_ref[0] * n_own + c, 0))
    return pl.pallas_call(
        out_body,
        grid_spec=pltpu.PrefetchScalarGridSpec(
            num_scalar_prefetch=1, grid=(n_e, n_own),
            in_specs=[row, row, pl.BlockSpec((1, f, d), lambda e, c, q_ref: (e + off, 0, 0))],
            out_specs=pl.BlockSpec((1, m, d), lambda e, c, q_ref: (e, c, 0))),
        out_shape=jax.ShapeDtypeStruct((n_e, n_own * m, d), BF), compiler_params=params(2),
        cost_estimate=cost(2 * n_e * n_own * m * d * f, 2 * n_e * n_own * m * (d + 2 * f)), name="own_out",
    )(q, a, b, w2)


def back_of(do, a_ref, b_ref, w2):
    dh = dot(do, w2, 1, 1)
    a = a_ref[0].astype(F32)
    b = b_ref[0].astype(F32)
    sig = jax.nn.sigmoid(a)
    act = a * sig
    h = (act * b).astype(BF)
    db = (dh * a * sig).astype(BF)
    da = (dh * b * sig * (1.0 + a * (1.0 - sig))).astype(BF)
    return h, da, db


def own_back_body(q_ref, do_ref, a_ref, b_ref, w1_ref, w3_ref, w2_ref, dx_ref):
    _, da, db = back_of(do_ref[0], a_ref, b_ref, w2_ref[0])
    dx_ref[0] = (dot(da, w1_ref[0], 1, 1) + dot(db, w3_ref[0], 1, 1)).astype(BF)


def own_back(q, do, a, b, w1, w3, w2, m, n_own, off):
    n_e, _, f = a.shape
    d = w2.shape[2]
    row = lambda width: pl.BlockSpec((1, m, width), lambda e, c, q_ref: (e, q_ref[0] * n_own + c, 0))
    wsp = lambda s: pl.BlockSpec((1,) + s.shape[1:], lambda e, c, q_ref: (e + off, 0, 0))
    return pl.pallas_call(
        own_back_body,
        grid_spec=pltpu.PrefetchScalarGridSpec(
            num_scalar_prefetch=1, grid=(n_e, n_own),
            in_specs=[row(d), row(f), row(f), wsp(w1), wsp(w3), wsp(w2)],
            out_specs=pl.BlockSpec((1, m, d), lambda e, c, q_ref: (e, c, 0))),
        out_shape=jax.ShapeDtypeStruct((n_e, n_own * m, d), BF), compiler_params=params(2),
        cost_estimate=cost(6 * n_e * n_own * m * d * f, 2 * n_e * n_own * m * (2 * d + 2 * f)), name="own_back",
    )(q, do, a, b, w1, w3, w2)


def combine_body(caps, gated, slot_ref, *refs):
    if gated:
        gate_ref, hot_ref, cold_ref, y_ref = refs
    else:
        hot_ref, cold_ref, y_ref = refs
    n_rows = sum(caps)
    tok_n = y_ref.shape[0]
    col = lax.broadcasted_iota(jnp.int32, (tok_n, n_rows), 1)
    weight = jnp.zeros((tok_n, n_rows), F32)
    for i in range(len(caps)):
        gate = gate_ref[0, :, i:i + 1] if gated else 1.0
        weight = jnp.where(col == slot_ref[0, :, i:i + 1], gate, weight)
    terms = [weight.astype(BF)]
    if gated:
        rest = weight - terms[0].astype(F32)
        terms.append(rest.astype(BF))
        terms.append((rest - terms[1].astype(F32)).astype(BF))
    width = 256
    for n in range(y_ref.shape[1] // width):
        cols = pl.ds(n * width, width)
        rows = jnp.concatenate(
            [hot_ref[0, :, cols].astype(F32)] + [cold_ref[i, 0, :, cols].astype(F32) for i in range(len(caps) - 1)],
            axis=0).astype(BF)
        total = dot(terms[0], rows)
        for term in terms[1:]:
            total = total + dot(term, rows)
        y_ref[:, cols] = total


def combine(caps, slot, gate, hot, cold):
    n_src, cap_hot, d = hot.shape
    tok_n = slot.shape[1]
    n_loc = len(caps)
    table = pl.BlockSpec((1, tok_n, n_loc), lambda s: (s, 0, 0))
    tables = [slot] + ([gate] if gate is not None else [])
    return pl.pallas_call(
        functools.partial(combine_body, caps, gate is not None),
        grid=(n_src,),
        in_specs=[table] * len(tables) + [
            pl.BlockSpec((1, cap_hot, d), lambda s: (s, 0, 0)),
            pl.BlockSpec((n_loc - 1, 1, caps[1], d), lambda s: (0, s, 0, 0))],
        out_specs=pl.BlockSpec((tok_n, d), lambda s: (s, 0)),
        out_shape=jax.ShapeDtypeStruct((n_src * tok_n, d), F32), compiler_params=params(1),
        cost_estimate=cost((6 if gate is not None else 2) * n_src * tok_n * sum(caps) * d,
                           n_src * d * (4 * tok_n + 2 * sum(caps))),
        name="combine_y" if gate is not None else "combine_dx",
    )(*tables, hot, cold)


def hot_grad_body(x_ref, do_ref, a_ref, b_ref, w2_ref, g1_ref, g3_ref, g2_ref):
    h, da, db = back_of(do_ref[0], a_ref, b_ref, w2_ref[0])
    x = x_ref[0]
    parts = dot(x, da, 0, 0), dot(x, db, 0, 0), dot(h, do_ref[0], 0, 0)

    @pl.when(pl.program_id(0) == 0)
    def _():
        for ref, part in zip((g1_ref, g3_ref, g2_ref), parts):
            ref[0] = part

    @pl.when(pl.program_id(0) > 0)
    def _():
        for ref, part in zip((g1_ref, g3_ref, g2_ref), parts):
            ref[0] += part


def hot_grads(x, do, a, b, w1, w2, m):
    n_r, d = x.shape[1:]
    f = a.shape[2]
    row = lambda width: pl.BlockSpec((1, m, width), lambda c: (0, c, 0))
    first = lambda s: pl.BlockSpec((1,) + s.shape[1:], lambda c: (0, 0, 0))
    shapes = [jax.ShapeDtypeStruct(w1.shape, F32), jax.ShapeDtypeStruct(w1.shape, F32),
              jax.ShapeDtypeStruct(w2.shape, F32)]
    return pl.pallas_call(
        hot_grad_body, grid=(n_r // m,), in_specs=[row(d), row(d), row(f), row(f), first(w2)],
        out_specs=[first(s) for s in shapes], out_shape=shapes, compiler_params=params(1),
        cost_estimate=cost(8 * n_r * d * f, 2 * n_r * (2 * d + 2 * f)), name="hot_grads",
    )(x, do, a, b, w2)


def cold_grad_body(n_chunk, *refs):
    (chunk_ref, a_ref, b_ref, w2_ref, x_ref, do_ref, _, _, _, g1_ref, g3_ref, g2_ref, h_s, da_s, db_s) = refs
    step = pl.program_id(1)
    m = chunk_ref.shape[1]

    @pl.when(step < n_chunk)
    def _():
        h, da, db = back_of(chunk_ref[0], a_ref, b_ref, w2_ref[0])
        rows = pl.ds(pl.multiple_of(step * m, m), m)
        h_s[rows, :] = h
        da_s[rows, :] = da
        db_s[rows, :] = db

    @pl.when(step >= n_chunk)
    def _():
        x = x_ref[0]
        g1_ref[0] = dot(x, da_s[...], 0, 0)
        g3_ref[0] = dot(x, db_s[...], 0, 0)
        g2_ref[0] = dot(h_s[...], do_ref[0], 0, 0)


def cold_grads(grads, x, do, a, b, w2, m, tile, off):
    n_e, n_r, d = x.shape
    f = a.shape[2]
    n_chunk, n_tile = n_r // m, d // tile
    chunk = lambda width: pl.BlockSpec((1, m, width), lambda e, s: (e, jnp.minimum(s, n_chunk - 1), 0))
    place = lambda s: jnp.maximum(s - n_chunk, 0)
    tiles = pl.BlockSpec((1, n_r, tile), lambda e, s: (e, 0, place(s)))
    any_spec = pl.BlockSpec(memory_space=pl.ANY)
    rows_out = pl.BlockSpec((1, tile, f), lambda e, s: (e + off, place(s), 0))
    cols_out = pl.BlockSpec((1, f, tile), lambda e, s: (e + off, 0, place(s)))
    return pl.pallas_call(
        functools.partial(cold_grad_body, n_chunk),
        grid=(n_e, n_chunk + n_tile),
        in_specs=[chunk(d), chunk(f), chunk(f), pl.BlockSpec((1, f, d), lambda e, s: (e + off, 0, 0)),
                  tiles, tiles, any_spec, any_spec, any_spec],
        out_specs=[rows_out, rows_out, cols_out],
        out_shape=[jax.ShapeDtypeStruct(g.shape, F32) for g in grads],
        scratch_shapes=[pltpu.VMEM((n_r, f), BF)] * 3,
        input_output_aliases={6: 0, 7: 1, 8: 2}, compiler_params=params(2),
        cost_estimate=cost(8 * n_e * n_r * d * f, 2 * n_e * n_r * (3 * d + 2 * f)), name="cold_grads",
    )(do, a, b, w2, x, do, *grads)


def solution(mesh):
    n_dev = mesh.shape['expert']
    n_data = mesh.shape['data']
    row_spec = P(('pod', 'data', 'expert'), None)
    w_spec = P('expert', None, None)
    grad_spec = P(('pod', 'expert'), None, None)
    both = ('data', 'expert')

    def body(tokens, routes, gates, grad_y, w_in1, w_in3, w_out):
        tok_n, d_model = tokens.shape
        top_k = routes.shape[1]
        n_loc = w_in1.shape[0]
        n_exp = n_loc * n_dev
        n_src = n_data * n_dev
        cap_cold, cap_hot = value_a10(tok_n, top_k, n_exp)
        assert (n_exp // 2) % n_loc == 0
        caps = (cap_hot,) + (cap_cold,) * (n_loc - 1)
        offs = [0] + [cap_hot + i * cap_cold for i in range(n_loc - 1)]
        q = lax.axis_index('data')
        q_arr = jnp.reshape(q, (1,)).astype(jnp.int32)

        local = jnp.concatenate([routes.T.astype(F32), gates.T], axis=0)
        tables = lax.all_gather(local, both, axis=0, tiled=True).reshape(n_src, 2 * top_k, tok_n)
        x_all = lax.all_gather(tokens, both, axis=0, tiled=True).reshape(n_src, tok_n, d_model)
        dy_all = lax.all_gather(grad_y, both, axis=0, tiled=True).reshape(n_src, tok_n, d_model)
        ids = lax.axis_index('expert') * n_loc + jnp.arange(n_loc)
        match = tables[:, :top_k, None, :] == ids.astype(F32)[None, None, :, None]
        hit = jnp.any(match, axis=1)
        gate = jnp.sum(jnp.where(match, tables[:, top_k:, None, :], 0.0), axis=1)
        before = (jnp.arange(tok_n)[:, None] < jnp.arange(tok_n)[None, :]).astype(BF)
        rank = jnp.einsum('sit,tu->siu', hit.astype(BF), before, preferred_element_type=F32).astype(jnp.int32)
        cap_here = jnp.where((ids == 0) | (ids == n_exp // 2), cap_hot, cap_cold)
        rank = jnp.where(hit & (rank < cap_here[None, :, None]), rank, -1)
        own = lambda t: lax.dynamic_slice_in_dim(t, q * n_dev, n_dev, 0).transpose(0, 2, 1)
        rank_own = own(rank)
        slot_own = jnp.where(rank_own >= 0, rank_own + jnp.array(offs, jnp.int32), -1)
        gate_own = own(gate)

        m_cold, m_hot = n_dev * cap_cold, n_dev * cap_hot // 2
        xh, xc = gather_rows(caps, rank, None, x_all)
        xh = xh.reshape(1, n_src * cap_hot, d_model)
        xc = xc.reshape(n_loc - 1, n_src * cap_cold, d_model)
        ac, bc = expert_in(xc, w_in1, w_in3, m_cold, 1)
        ah, bh = expert_in(xh, w_in1, w_in3, m_hot, 0)
        oc = own_out(q_arr, ac, bc, w_out, m_cold, 1, 1).reshape(n_loc - 1, n_dev, cap_cold, d_model)
        oh = own_out(q_arr, ah, bh, w_out, m_hot, 2, 0).reshape(n_dev, cap_hot, d_model)
        y_part = combine(caps, slot_own, gate_own, oh, oc)
        y_out = lax.psum_scatter(y_part, 'expert', scatter_dimension=0, tiled=True).astype(BF)

        doh, doc = gather_rows(caps, rank, gate, dy_all)
        doh = doh.reshape(1, n_src * cap_hot, d_model)
        doc = doc.reshape(n_loc - 1, n_src * cap_cold, d_model)
        dxc = own_back(q_arr, doc, ac, bc, w_in1, w_in3, w_out, m_cold, 1, 1)
        dxh = own_back(q_arr, doh, ah, bh, w_in1, w_in3, w_out, m_hot, 2, 0)
        dx_part = combine(caps, slot_own, None, dxh.reshape(n_dev, cap_hot, d_model),
                          dxc.reshape(n_loc - 1, n_dev, cap_cold, d_model))
        grad_x = lax.psum_scatter(dx_part, 'expert', scatter_dimension=0, tiled=True).astype(BF)

        grads = hot_grads(xh, doh, ah, bh, w_in1, w_out, m_hot)
        grads = cold_grads(grads, xc, doc, ac, bc, w_out, m_cold, d_model // 3, 1)
        return (y_out, grad_x) + tuple(grads)

    return jax.shard_map(body, mesh=mesh,
                         in_specs=(row_spec, row_spec, row_spec, row_spec, w_spec, w_spec, w_spec),
                         out_specs=(row_spec, row_spec, grad_spec, grad_spec, grad_spec),
                         check_vma=False)
```

time: 1620 us -> 706 us (0.44)
  waiting for transfers between devices: 791 us -> 162 us
  Pallas kernels: 0 us -> 474 us
  local copies, waits for them, and re-layouts: 440 us -> 19.6 us
  matrix products: 174 us -> 0.98 us
  other arithmetic: 160 us -> 22.7 us
  starting transfers between devices: 29.3 us -> 0.31 us
    pallas_call x0 -> x12, Pallas kernels: none -> 474 us  [the longest x1 112 us: cold_grads(): pl.pallas_call(functools.partial(cold_grad_body, n_chunk), grid=(n_e, n_c...]
    all_to_all x4 -> x0, waiting for transfers between devices: 405 us -> none  [the longest x1 160 us: body(): back_dx = lax.all_to_all(cold_dx, 'expert', 1, 0, tiled=True)]
    psum x3 -> x0, waiting for transfers between devices: 386 us -> none  [the longest x1 182 us: body(): lax.psum((owned_copy(w_in1), owned_copy(w_in3), owned_copy(w_out)), 'expe...]
    dot_general x18 -> x1, matrix products: 174 us -> 0.98 us  [body(): jnp.einsum('sit,tu->siu', hit.astype(BF), before, preferred_element_type=...]
    gather x12 -> x0, local copies, waits for them, and re-layouts: 162 us -> none  [the longest x2 63.1 us: combine(): jnp.take(cold_vals, cold_rows, axis=0, mode='fill', fill_value=0)]
    all_gather x0 -> x3, waiting for transfers between devices: none -> 160 us  [the longest x1 119 us: body(): lax.all_gather(tokens, both, axis=0, tiled=True)]
    unnamed x72 -> x5, local copies, waits for them, and re-layouts: 87.1 us -> 2.75 us
    scatter x5 -> x0, local copies, waits for them, and re-layouts: 77.8 us -> none  [the longest x2 31.3 us: gather_rows(): jnp.zeros((n_rows,), jnp.float32).at[slot_rows].set(gate_flat, mode='drop')]
  transfers between devices with their start and end apart: 7 -> 5, of which waited for: 6 -> 2; matrix products, arithmetic and copies ran while one was open for 35% -> 5% of each run, Pallas kernels for 0% -> 68%
where the time goes in v1:
time: 706 us; the launch traced here: 694 us
  Pallas kernels  474 us (67%)
  waiting for transfers between devices  162 us (23%)
  other arithmetic  22.7 us (3%)
  local copies, waits for them, and re-layouts  19.6 us (3%)
  between operations  14.3 us (2%)
    all_gather x1, waiting for transfers between devices, body(): lax.all_gather(tokens, both, axis=0, tiled=True)  119 us
    pallas_call x1, Pallas kernels, cold_grads(): pl.pallas_call(functools.partial(cold_grad_body, n_chunk), grid=(n_e, n_c...  112 us
    pallas_call x2, Pallas kernels, gather_rows(): pl.pallas_call(functools.partial(gather_body, caps, gate is not None), gr...  109 us
    pallas_call x2, Pallas kernels, expert_in(): pl.pallas_call(fwd_body, grid=(n_e, n_r // m), in_specs=[row(d), wsp, wsp...  74.4 us
    pallas_call x2, Pallas kernels, combine(): pl.pallas_call(functools.partial(combine_body, caps, gate is not None), g...  64.1 us
    pallas_call x1, Pallas kernels, hot_grads(): pl.pallas_call(hot_grad_body, grid=(n_r // m,), in_specs=[row(d), row(d),...  60 us
    all_gather x1, waiting for transfers between devices, body(): lax.all_gather(local, both, axis=0, tiled=True)  41.3 us
    pallas_call x2, Pallas kernels, own_back(): pl.pallas_call(own_back_body, grid_spec=pltpu.PrefetchScalarGridSpec(num_...  37.3 us
  transfers between devices with their start and end apart: 5, of which 2 were waited for; matrix products, arithmetic and copies ran while one was open for 5% of the time, Pallas kernels for 68%

profile of v1, /device:TPU:97, one launch (start us, length us, event | category | flops | bytes accessed | tf_op | source)
XLA Modules:
  0.0 694.0 jit_solution(29361486355205667)
XLA Ops:
  7.2 0.1 all-gather.4.cloned.1.call-start
  7.2 0.7 convert_bitcast_fusion
  8.0 1.3 pad_maximum_fusion
  9.3 0.1 all-gather.4.cloned.1.call-update
  9.4 0.1 all-gather.6.cloned.1.call-start
  9.4 0.7 all-gather.6.cloned.1.call-update
  10.2 0.1 all-gather.8.cloned.1.call-start
  10.2 0.7 all-gather.8.cloned.1.call-update
  11.0 0.1 reduce-scatter.3.cloned.1.call-start
  11.1 41.3 %all-gather.4.cloned.1.call-done = f32[512,512]{1,0:T(8,128)} async-done(((f32[16,512]{1,0:T(8,128)}), f32[512,512]{1,0:T(8,128)}) %all-gather.4.cloned.1.call-update) | async-done | bytes 1048592 | tf_op jit(solution)/shard_map/all_gather | solution.py:303
  52.4 1.3 fusion.7
  53.6 1.0 compare_reduce_fusion
  54.6 3.7 copy.23
  58.4 1.0 fusion.3
  59.4 5.8 copy.22
  65.2 1.0 fusion.1.refs_0_
  66.2 0.0 copy-start
  66.2 0.8 copy-done
  67.0 2.0 copy.27
  69.0 9.0 %convert_select_fusion = s32[32,5,512]{1,2,0:T(8,128)} fusion(f32[32,5,512]{1,2,0:T(8,128)} %copy.22, pred[32,5,512]{1,2,0:T(8,128)(4,1)S(1)} %copy.23, s32[5]{0:T(128)S(1)} %or_select_fusion), kind=kLoop, calls=%fused_computation | loop fusion | flops 327680 | bytes 737300 | tf_op jit(solution)/shard_map/jit(_where)/select_n | solution.py:313
  78.0 0.0 copy-start.1
  78.0 6.0 copy.25.rank_ref
  84.0 0.0 copy-done.1
  84.0 3.1 select_bitcast_fusion.slot_ref
  87.1 118.9 %all-gather.6.cloned.1.call-done = bf16[16384,1536]{1,0:T(8,128)(2,1)} async-done(((bf16[512,1536]{1,0:T(8,128)(2,1)}), bf16[16384,1536]{1,0:T(8,128)(2,1)}) %all-gather.6.cloned.1.call-update) | async-done | bytes 50331664 | tf_op jit(solution)/shard_map/all_gather | solution.py:304
  206.0 53.6 %gather_x.1 = (bf16[32,192,1536]{2,1,0:T(8,128)(2,1)}, bf16[4,32,104,1536]{3,2,1,0:T(8,128)(2,1)}) custom-call(s32[32,5,512]{2,1,0:T(8,128)} %copy.25.rank_ref, bf16[32,512,1536]{2,1,0:T(8,128)(2,1)} %bitcast.34), custom_call_target="tpu_custom_call" | custom-call | flops 30601641984 | bytes 110100480 | tf_op jit(solution)/shard_map/gather_x/pallas_call | solution.py:69
  259.6 24.4 %expert_in.2 = (bf16[1,6144,512]{2,1,0:T(8,128)(2,1)}, bf16[1,6144,512]{2,1,0:T(8,128)(2,1)}) custom-call(bf16[1,6144,1536]{2,1,0:T(8,128)(2,1)} %bitcast.37, bf16[5,1536,512]{2,1,0:T(8,128)(2,1)} %w1_ref.7, bf16[5,1536,512]{2,1,0:T(8,128)(2,1)} %w3_ref.7), custom_call_target="tpu_custom_call" | custom-call | flops 19327352832 | bytes 31457280 | tf_op jit(solution)/shard_map/expert_in/pallas_call | solution.py:94
  284.1 6.2 own_out.2
  290.2 50.0 %expert_in.3 = (bf16[4,3328,512]{2,1,0:T(8,128)(2,1)}, bf16[4,3328,512]{2,1,0:T(8,128)(2,1)}) custom-call(bf16[4,3328,1536]{2,1,0:T(8,128)(2,1)} %bitcast.35, bf16[5,1536,512]{2,1,0:T(8,128)(2,1)} %w1_ref.7, bf16[5,1536,512]{2,1,0:T(8,128)(2,1)} %w3_ref.7), custom_call_target="tpu_custom_call" | custom-call | flops 41875931136 | bytes 68157440 | tf_op jit(solution)/shard_map/expert_in/pallas_call | solution.py:94
  340.2 11.8 %own_out.3 = bf16[4,832,1536]{2,1,0:T(8,128)(2,1)} custom-call(s32[1]{0:T(128)} %bitcast.6.q_ref, bf16[4,3328,512]{2,1,0:T(8,128)(2,1)} %get-tuple-element.23.a_ref.refs_1_, bf16[4,3328,512]{2,1,0:T(8,128)(2,1)} %get-tuple-element.24.b_ref.refs_2_, bf16[5,512,1536]{2,1,0:T(8,128)(2,1)} %refs_3_.1), custom_call_target="tpu_custom_call" | custom-call | flops 5234491392 | bytes 17039360 | tf_op jit(solution)/shard_map/own_out/pallas_call | solution.py:114
  352.0 42.5 %combine_y.1 = f32[4096,1536]{1,0:T(8,128)} custom-call(s32[8,512,5]{2,1,0:T(8,128)} %select_bitcast_fusion.slot_ref, f32[8,512,5]{2,1,0:T(8,128)} %bitcast.30, bf16[8,192,1536]{2,1,0:T(8,128)(2,1)} %bitcast.29, bf16[4,8,104,1536]{3,2,1,0:T(8,128)(2,1)} %bitcast.28), custom_call_target="tpu_custom_call" | custom-call | flops 22951231488 | bytes 40108032 | tf_op jit(solution)/shard_map/combine_y/pallas_call | solution.py:193
  394.5 0.1 reduce-scatter.3.cloned.1.call-update
  394.5 0.1 reduce-scatter.5.cloned.1.call-start
  394.6 0.0 all-gather.8.cloned.1.call-done
  394.6 55.0 %gather_do.1 = (bf16[32,192,1536]{2,1,0:T(8,128)(2,1)}, bf16[4,32,104,1536]{3,2,1,0:T(8,128)(2,1)}) custom-call(s32[32,5,512]{2,1,0:T(8,128)} %copy.25.rank_ref, f32[32,5,512]{2,1,0:T(8,128)} %copy-done, bf16[32,512,1536]{2,1,0:T(8,128)(2,1)} %bitcast.33), custom_call_target="tpu_custom_call" | custom-call | flops 30601641984 | bytes 110100480 | tf_op jit(solution)/shard_map/gather_do/pallas_call | solution.py:69
  449.6 13.7 %own_back.2 = bf16[1,1536,1536]{2,1,0:T(8,128)(2,1)} custom-call(s32[1]{0:T(128)} %bitcast.6.q_ref, bf16[1,6144,1536]{2,1,0:T(8,128)(2,1)} %bitcast.26, bf16[1,6144,512]{2,1,0:T(8,128)(2,1)} %get-tuple-element.20.a_ref, bf16[1,6144,512]{2,1,0:T(8,128)(2,1)} %get-tuple-element.21.b_ref, bf16[5,1536,512]{2,1,0:T(8,128)(2,1)} %w1_ref.7, ...), custom_call_target="tpu_custom_call" | custom-call | flops 7247757312 | bytes 12582912 | tf_op jit(solution)/shard_map/own_back/pallas_call | solution.py:147
  463.4 23.6 %own_back.3 = bf16[4,832,1536]{2,1,0:T(8,128)(2,1)} custom-call(s32[1]{0:T(128)} %bitcast.6.q_ref, bf16[4,3328,1536]{2,1,0:T(8,128)(2,1)} %bitcast.21, bf16[4,3328,512]{2,1,0:T(8,128)(2,1)} %get-tuple-element.23.a_ref.refs_1_, bf16[4,3328,512]{2,1,0:T(8,128)(2,1)} %get-tuple-element.24.b_ref.refs_2_, bf16[5,1536,512]{2,1,0:T(8,128)(2,1)} %w1_ref.7, ...), custom_call_target="tpu_custom_call" | custom-call | flops 15703474176 | bytes 27262976 | tf_op jit(solution)/shard_map/own_back/pallas_call | solution.py:147
  487.0 21.5 %combine_dx.1 = f32[4096,1536]{1,0:T(8,128)} custom-call(s32[8,512,5]{2,1,0:T(8,128)} %select_bitcast_fusion.slot_ref, bf16[8,192,1536]{2,1,0:T(8,128)(2,1)} %bitcast.25, bf16[4,8,104,1536]{3,2,1,0:T(8,128)(2,1)} %bitcast.24), custom_call_target="tpu_custom_call" | custom-call | flops 7650410496 | bytes 40108032 | tf_op jit(solution)/shard_map/combine_dx/pallas_call | solution.py:193
  508.5 0.1 reduce-scatter.5.cloned.1.call-update
  508.6 60.0 %hot_grads.1 = (f32[5,1536,512]{2,1,0:T(8,128)}, f32[5,1536,512]{2,1,0:T(8,128)}, f32[5,512,1536]{2,1,0:T(8,128)}) custom-call(bf16[1,6144,1536]{2,1,0:T(8,128)(2,1)} %bitcast.38, bf16[1,6144,1536]{2,1,0:T(8,128)(2,1)} %bitcast.27, bf16[1,6144,512]{2,1,0:T(8,128)(2,1)} %get-tuple-element.20.a_ref, bf16[1,6144,512]{2,1,0:T(8,128)(2,1)} %get-tuple-element.21.b_ref, ...), custom_call_target="tpu_custom_call" | custom-call | flops 38654705664 | bytes 50331648 | tf_op jit(solution)/shard_map/hot_grads/pallas_call | solution.py:230
  568.6 112.0 %cold_grads.1 = (f32[5,1536,512]{2,1,0:T(8,128)}, f32[5,1536,512]{2,1,0:T(8,128)}, f32[5,512,1536]{2,1,0:T(8,128)}) custom-call(bf16[4,3328,1536]{2,1,0:T(8,128)(2,1)} %bitcast.22, bf16[4,3328,512]{2,1,0:T(8,128)(2,1)} %get-tuple-element.23.a_ref.refs_1_, ...), custom_call_target="tpu_custom_call", output_to_operand_aliasing={{0}: (6, {}), {1}: (7, {}), {2}: (8, {})} | custom-call | flops 83751862272 | bytes 149946368 | tf_op jit(solution)/shard_map/cold_grads/pallas_call | solution.py:268
  680.6 0.0 reduce-scatter.3.cloned.1.call-done
  680.6 3.2 convert_element_type.28
  683.9 0.0 reduce-scatter.5.cloned.1.call-done
  683.9 3.2 convert_element_type.29
  (3 shorter events, 0.0 us)
Async XLA Ops:
  7.2 45.2 %all-gather.4.cloned.1.call-start = ((), (), s32[]{:S(2)}) async-start(), calls=%async_computation.2 | async-start | bytes 1081344 | tf_op jit(solution)/shard_map/all_gather | solution.py:303
  9.4 196.6 %all-gather.6.cloned.1.call-start = ((), (), s32[]{:S(2)}) async-start(), calls=%async_computation.3 | async-start | bytes 51904512 | tf_op jit(solution)/shard_map/all_gather | solution.py:304
  10.2 384.5 %all-gather.8.cloned.1.call-start = ((), (), s32[]{:S(2)}) async-start(), calls=%async_computation.5 | async-start | bytes 51904512 | tf_op jit(solution)/shard_map/all_gather | solution.py:305
  11.0 669.7 %reduce-scatter.3.cloned.1.call-start = ((), (), s32[]{:S(2)}) async-start(), calls=%async_computation.4 | async-start | bytes 28311552 | tf_op jit(solution)/shard_map/reduce_scatter | solution.py:328
  66.2 0.8 copy-start
  78.0 6.0 copy-start.1
  394.5 289.3 %reduce-scatter.5.cloned.1.call-start = ((), (), s32[]{:S(2)}) async-start(), calls=%async_computation.6 | async-start | bytes 28311552 | tf_op jit(solution)/shard_map/reduce_scatter | solution.py:337
Sparse Core Ops, SparseCore 0:
  10.7 41.6 all-gather.3
  54.4 151.5 all-gather.5
  208.1 151.2 all-gather.7
  394.7 127.1 reduce-scatter.2
  524.0 128.5 reduce-scatter.4

commit v2 on v1

v2 whole, which is shorter than its diff:
```python
import functools

import jax
import jax.numpy as jnp
from jax import lax
from jax.experimental import pallas as pl
from jax.experimental.pallas import tpu as pltpu
from jax.sharding import PartitionSpec as P

N_HOT = 2
BF = jnp.bfloat16
F32 = jnp.float32
VMEM_LIMIT = 60 * 1024 * 1024


def value_a10(tok_dev, top_k, n_exp):
    cap_hot = 3 * tok_dev // 8
    cap_cold = max(8, ((tok_dev * top_k - N_HOT * cap_hot) // (n_exp - N_HOT) + 7) // 8 * 8)
    return cap_cold, cap_hot


def dot(a, b, ca=1, cb=0):
    return lax.dot_general(a, b, (((ca,), (cb,)), ((), ())), preferred_element_type=F32)


def params(n_axes):
    return pltpu.CompilerParams(dimension_semantics=("arbitrary",) * n_axes, vmem_limit_bytes=VMEM_LIMIT)


def cost(flops, nbytes):
    return pl.CostEstimate(flops=int(flops), bytes_accessed=int(nbytes), transcendentals=0)


def gather_body(caps, gated, n_half, rank_ref, *refs):
    if gated:
        gate_ref, src_ref, rows_ref, buf, sem = refs
    else:
        src_ref, rows_ref, buf, sem = refs
    step = pl.program_id(0)
    n_src_step, tok_n, d = src_ref.shape
    blk = caps[-1]
    slot = lax.rem(step, 2)

    def copies(step_i, slot_i):
        out = []
        for k in range(n_src_step):
            s = step_i * n_src_step + k
            half = s // n_half
            out.append(pltpu.make_async_copy(
                buf.at[slot_i, k, pl.ds(0, 2)], rows_ref.at[half, pl.ds(2 * (s - half * n_half), 2)], sem.at[slot_i]))
            out.append(pltpu.make_async_copy(
                buf.at[slot_i, k, pl.ds(2, len(caps) - 1)], rows_ref.at[pl.ds(2, len(caps) - 1), s], sem.at[slot_i]))
        return out

    @pl.when(step >= 2)
    def _():
        for c in copies(step - 2, slot):
            c.wait()

    for k in range(n_src_step):
        picks, scales = [], []
        for i, cap in enumerate(caps):
            hit = lax.broadcasted_iota(jnp.int32, (cap, tok_n), 0) == rank_ref[k, i:i + 1, :]
            picks.append(jnp.where(hit, 1.0, 0.0))
            if gated:
                scales.append(jnp.sum(jnp.where(hit, gate_ref[k, i:i + 1, :], 0.0), axis=1, keepdims=True))
        pick = jnp.concatenate(picks, axis=0).astype(BF)
        scale = jnp.concatenate(scales, axis=0) if gated else None
        width = 256
        for n in range(d // width):
            cols = pl.ds(n * width, width)
            rows = dot(pick, src_ref[k, :, cols])
            if gated:
                rows = rows * scale
            for j in range(sum(caps) // blk):
                buf[slot, k, j, :, cols] = rows[j * blk:(j + 1) * blk].astype(BF)

    for c in copies(step, slot):
        c.start()

    @pl.when(step == pl.num_programs(0) - 1)
    def _():
        for c in copies(step - 1, 1 - slot):
            c.wait()
        for c in copies(step, slot):
            c.wait()


def gather_rows(caps, rank, gate, src):
    n_src, tok_n, d = src.shape
    n_loc = len(caps)
    blk = caps[-1]
    per = 2
    assert caps[0] == 2 * blk and n_src % (2 * per) == 0 and n_src // per >= 2
    table = pl.BlockSpec((per, n_loc, tok_n), lambda s: (s, 0, 0))
    ins = [rank] + ([gate] if gate is not None else []) + [src]
    return pl.pallas_call(
        functools.partial(gather_body, caps, gate is not None, n_src // 2),
        grid=(n_src // per,),
        in_specs=[table] * (len(ins) - 1) + [pl.BlockSpec((per, tok_n, d), lambda s: (s, 0, 0))],
        out_specs=pl.BlockSpec(memory_space=pl.ANY),
        out_shape=jax.ShapeDtypeStruct((n_loc + 1, n_src, blk, d), BF),
        scratch_shapes=[pltpu.VMEM((2, per, n_loc + 1, blk, d), BF), pltpu.SemaphoreType.DMA((2,))],
        compiler_params=params(1),
        cost_estimate=cost(2 * n_src * sum(caps) * tok_n * d, 2 * n_src * d * (tok_n + sum(caps))),
        name="gather_do" if gate is not None else "gather_x",
    )(*ins).reshape(n_loc + 1, n_src * blk, d)


def own_chunk(i, q, n_chunk):
    hot = i < 2
    return jnp.where(hot, 2 * q // n_chunk, i), jnp.where(hot, 2 * q % n_chunk + i, q)


def expert_of(e):
    return jnp.maximum(e - 1, 0)


def fwd_body(n_chunk, q_ref, x_ref, w1_ref, w3_ref, w2_ref, a_ref, b_ref, o_ref):
    e, c, q = pl.program_id(0), pl.program_id(1), q_ref[0]
    x = x_ref[0]
    a_ref[0] = dot(x, w1_ref[0]).astype(BF)
    b_ref[0] = dot(x, w3_ref[0]).astype(BF)
    own = jnp.where(e < 2, e * n_chunk + c - 2 * q, jnp.where(c == q, 0, 2))

    @pl.when((own == 0) | (own == 1))
    def _():
        a = a_ref[0].astype(F32)
        h = (a * jax.nn.sigmoid(a) * b_ref[0].astype(F32)).astype(BF)
        o_ref[0] = dot(h, w2_ref[0]).astype(BF)


def expert_in(q, x_rows, w1, w3, w2, m):
    n_e, n_r, d = x_rows.shape
    f = w1.shape[2]
    row = lambda width: pl.BlockSpec((1, m, width), lambda e, c, q_ref: (e, c, 0))
    wsp = lambda s: pl.BlockSpec((1,) + s.shape[1:], lambda e, c, q_ref: (expert_of(e), 0, 0))

    n_chunk = n_r // m

    def out_slot(e, c, q_ref):
        return (jnp.where(e < 2, jnp.clip(e * n_chunk + c - 2 * q_ref[0], 0, 1), e), 0, 0)

    return pl.pallas_call(
        functools.partial(fwd_body, n_chunk),
        grid_spec=pltpu.PrefetchScalarGridSpec(
            num_scalar_prefetch=1, grid=(n_e, n_chunk), in_specs=[row(d), wsp(w1), wsp(w3), wsp(w2)],
            out_specs=[row(f), row(f), pl.BlockSpec((1, m, d), out_slot)]),
        out_shape=[jax.ShapeDtypeStruct((n_e, n_r, f), BF)] * 2 + [jax.ShapeDtypeStruct((n_e, m, d), BF)],
        compiler_params=params(2),
        cost_estimate=cost(4 * n_e * n_r * d * f, 2 * n_e * n_r * (d + 2 * f)), name="expert_in",
    )(q, x_rows, w1, w3, w2)


def back_of(do, a_ref, b_ref, w2):
    dh = dot(do, w2, 1, 1)
    a = a_ref[0].astype(F32)
    b = b_ref[0].astype(F32)
    sig = jax.nn.sigmoid(a)
    act = a * sig
    h = (act * b).astype(BF)
    db = (dh * a * sig).astype(BF)
    da = (dh * b * sig * (1.0 + a * (1.0 - sig))).astype(BF)
    return h, da, db


def own_back_body(q_ref, do_ref, a_ref, b_ref, w1_ref, w3_ref, w2_ref, dx_ref):
    _, da, db = back_of(do_ref[0], a_ref, b_ref, w2_ref[0])
    dx_ref[0] = (dot(da, w1_ref[0], 1, 1) + dot(db, w3_ref[0], 1, 1)).astype(BF)


def own_back(q, do, a, b, w1, w3, w2, m):
    n_e, _, f = a.shape
    d = w2.shape[2]
    n_chunk = a.shape[1] // m
    row = lambda width: pl.BlockSpec((1, m, width), lambda i, q_ref: own_chunk(i, q_ref[0], n_chunk) + (0,))
    wsp = lambda s: pl.BlockSpec((1,) + s.shape[1:], lambda i, q_ref: (expert_of(i), 0, 0))
    return pl.pallas_call(
        own_back_body,
        grid_spec=pltpu.PrefetchScalarGridSpec(
            num_scalar_prefetch=1, grid=(n_e,),
            in_specs=[row(d), row(f), row(f), wsp(w1), wsp(w3), wsp(w2)],
            out_specs=pl.BlockSpec((1, m, d), lambda i, q_ref: (i, 0, 0))),
        out_shape=jax.ShapeDtypeStruct((n_e, m, d), BF), compiler_params=params(1),
        cost_estimate=cost(6 * n_e * m * d * f, 2 * n_e * m * (2 * d + 2 * f)), name="own_back",
    )(q, do, a, b, w1, w3, w2)


def combine_body(caps, gated, slot_ref, *refs):
    n_loc = len(caps)
    gate_ref = refs[0] if gated else None
    row_refs, y_ref = refs[gated:gated + n_loc], refs[gated + n_loc]
    n_rows = sum(caps)
    tok_n = y_ref.shape[0]
    col = lax.broadcasted_iota(jnp.int32, (tok_n, n_rows), 1)
    weight = jnp.zeros((tok_n, n_rows), F32)
    for i in range(n_loc):
        gate = gate_ref[0, :, i:i + 1] if gated else 1.0
        weight = jnp.where(col == slot_ref[0, :, i:i + 1], gate, weight)
    terms = [weight.astype(BF)]
    if gated:
        rest = weight - terms[0].astype(F32)
        terms.append(rest.astype(BF))
        terms.append((rest - terms[1].astype(F32)).astype(BF))
    width = 256
    for n in range(y_ref.shape[1] // width):
        cols = pl.ds(n * width, width)
        rows = jnp.concatenate(
            [ref[0, j, :, cols].astype(F32) for ref in row_refs for j in range(ref.shape[1])], axis=0).astype(BF)
        total = dot(terms[0], rows)
        for term in terms[1:]:
            total = total + dot(term, rows)
        y_ref[:, cols] = total


def combine(caps, slot, gate, rows):
    n_src, tok_n, n_loc = slot.shape
    d = rows.shape[2]
    blk = caps[-1]
    rows = rows.reshape(n_loc + 1, n_src, blk, d)
    table = pl.BlockSpec((1, tok_n, n_loc), lambda s: (s, 0, 0))
    tables = [slot] + ([gate] if gate is not None else [])
    hot = pl.BlockSpec((1, 2, blk, d), lambda s: (s // (n_src // 2), s % (n_src // 2), 0, 0))
    colds = [pl.BlockSpec((1, 1, blk, d), lambda s, i=i: (2 + i, s, 0, 0)) for i in range(n_loc - 1)]
    return pl.pallas_call(
        functools.partial(combine_body, caps, gate is not None),
        grid=(n_src,),
        in_specs=[table] * len(tables) + [hot] + colds,
        out_specs=pl.BlockSpec((tok_n, d), lambda s: (s, 0)),
        out_shape=jax.ShapeDtypeStruct((n_src * tok_n, d), F32), compiler_params=params(1),
        cost_estimate=cost((6 if gate is not None else 2) * n_src * tok_n * sum(caps) * d,
                           n_src * d * (4 * tok_n + 2 * sum(caps))),
        name="combine_y" if gate is not None else "combine_dx",
    )(*tables, *([rows] * n_loc))


def grad_body(n_chunk, chunk_ref, a_ref, b_ref, w2_ref, x_ref, do_ref, g1_ref, g3_ref, g2_ref,
              h_s, da_s, db_s, acc):
    e, step = pl.program_id(0), pl.program_id(1)
    m = chunk_ref.shape[1]
    outs = (g1_ref, g3_ref, g2_ref)

    @pl.when(step < n_chunk)
    def _():
        h, da, db = back_of(chunk_ref[0], a_ref, b_ref, w2_ref[0])
        rows = pl.ds(pl.multiple_of(step * m, m), m)
        h_s[rows, :] = h
        da_s[rows, :] = da
        db_s[rows, :] = db

    @pl.when(step >= n_chunk)
    def _():
        x = x_ref[0]
        g1_ref[0] = dot(x, da_s[...], 0, 0)
        g3_ref[0] = dot(x, db_s[...], 0, 0)
        g2_ref[0] = dot(h_s[...], do_ref[0], 0, 0)
        tile = step - n_chunk

        @pl.when(e == 0)
        def _():
            for k, ref in enumerate(outs):
                acc[k, tile] = ref[0]

        @pl.when(e == 1)
        def _():
            for k, ref in enumerate(outs):
                ref[0] += acc[k, tile]


def expert_grads(x, do, a, b, w1, w2, m, tile):
    n_e, n_r, d = x.shape
    f = a.shape[2]
    assert tile == f
    n_chunk, n_tile = n_r // m, d // tile
    chunk = lambda width: pl.BlockSpec((1, m, width), lambda e, s: (e, jnp.minimum(s, n_chunk - 1), 0))
    place = lambda s: jnp.maximum(s - n_chunk, 0)
    tiles = pl.BlockSpec((1, n_r, tile), lambda e, s: (e, 0, place(s)))
    out_place = lambda e, s: jnp.where(e == 0, 0, place(s))
    rows_out = pl.BlockSpec((1, tile, f), lambda e, s: (expert_of(e), out_place(e, s), 0))
    cols_out = pl.BlockSpec((1, f, tile), lambda e, s: (expert_of(e), 0, out_place(e, s)))
    return pl.pallas_call(
        functools.partial(grad_body, n_chunk),
        grid=(n_e, n_chunk + n_tile),
        in_specs=[chunk(d), chunk(f), chunk(f), pl.BlockSpec((1, f, d), lambda e, s: (expert_of(e), 0, 0)),
                  tiles, tiles],
        out_specs=[rows_out, rows_out, cols_out],
        out_shape=[jax.ShapeDtypeStruct(w.shape, F32) for w in (w1, w1, w2)],
        scratch_shapes=[pltpu.VMEM((n_r, f), BF)] * 3 + [pltpu.VMEM((3, n_tile, tile, f), F32)],
        compiler_params=params(2),
        cost_estimate=cost(8 * n_e * n_r * d * f, 2 * n_e * n_r * (3 * d + 2 * f)), name="expert_grads",
    )(do, a, b, w2, x, do)


def solution(mesh):
    n_dev = mesh.shape['expert']
    n_data = mesh.shape['data']
    row_spec = P(('pod', 'data', 'expert'), None)
    w_spec = P('expert', None, None)
    grad_spec = P(('pod', 'expert'), None, None)
    both = ('data', 'expert')

    def body(tokens, routes, gates, grad_y, w_in1, w_in3, w_out):
        tok_n, d_model = tokens.shape
        top_k = routes.shape[1]
        n_loc = w_in1.shape[0]
        n_exp = n_loc * n_dev
        n_src = n_data * n_dev
        cap_cold, cap_hot = value_a10(tok_n, top_k, n_exp)
        assert (n_exp // 2) % n_loc == 0
        caps = (2 * cap_cold,) + (cap_cold,) * (n_loc - 1)
        assert cap_hot <= caps[0]
        offs = [0] + [(i + 2) * cap_cold for i in range(n_loc - 1)]
        q = lax.axis_index('data')
        q_arr = jnp.reshape(q, (1,)).astype(jnp.int32)

        routes_all = lax.all_gather(routes.T, both, axis=0, tiled=True).reshape(n_src, top_k, tok_n)
        gates_all = lax.all_gather(gates.T, both, axis=0, tiled=True).reshape(n_src, top_k, tok_n)
        x_all = lax.all_gather(tokens, both, axis=0, tiled=True).reshape(n_src, tok_n, d_model)
        dy_all = lax.all_gather(grad_y, both, axis=0, tiled=True).reshape(n_src, tok_n, d_model)
        ids = lax.axis_index('expert') * n_loc + jnp.arange(n_loc)
        match = routes_all[:, :, None, :] == ids[None, None, :, None]
        hit = jnp.any(match, axis=1)
        gate = jnp.sum(jnp.where(match, gates_all[:, :, None, :], 0.0), axis=1)
        before = (jnp.arange(tok_n)[:, None] < jnp.arange(tok_n)[None, :]).astype(BF)
        rank = jnp.einsum('sit,tu->siu', hit.astype(BF), before, preferred_element_type=F32).astype(jnp.int32)
        cap_here = jnp.where((ids == 0) | (ids == n_exp // 2), cap_hot, cap_cold)
        rank = jnp.where(hit & (rank < cap_here[None, :, None]), rank, -1)
        own = lambda t: lax.dynamic_slice_in_dim(t, q * n_dev, n_dev, 0).transpose(0, 2, 1)
        rank_own = own(rank)
        slot_own = jnp.where(rank_own >= 0, rank_own + jnp.array(offs, jnp.int32), -1)
        gate_own = own(gate)

        m = n_dev * cap_cold
        x_rows = gather_rows(caps, rank, None, x_all)
        a, b, o = expert_in(q_arr, x_rows, w_in1, w_in3, w_out, m)
        y_part = combine(caps, slot_own, gate_own, o)
        y_out = lax.psum_scatter(y_part, 'expert', scatter_dimension=0, tiled=True).astype(BF)

        do_rows = gather_rows(caps, rank, gate, dy_all)
        dx = own_back(q_arr, do_rows, a, b, w_in1, w_in3, w_out, m)
        dx_part = combine(caps, slot_own, None, dx)
        grad_x = lax.psum_scatter(dx_part, 'expert', scatter_dimension=0, tiled=True).astype(BF)

        grads = expert_grads(x_rows, do_rows, a, b, w_in1, w_out, m, w_in1.shape[2])
        return (y_out, grad_x) + tuple(grads)

    return jax.shard_map(body, mesh=mesh,
                         in_specs=(row_spec, row_spec, row_spec, row_spec, w_spec, w_spec, w_spec),
                         out_specs=(row_spec, row_spec, grad_spec, grad_spec, grad_spec),
                         check_vma=False)
```

time: 706 us -> 634 us (0.90); the launches traced: 694 us -> 632 us
  waiting for transfers between devices: 162 us -> 62.6 us
  blocking collectives: 0 us -> 68.8 us
  Pallas kernels: 474 us -> 449 us
    all_gather x0 -> x2, blocking collectives: none -> 68.8 us  [the longest x1 34.4 us: body(): lax.all_gather(gates.T, both, axis=0, tiled=True)]
    all_gather x1, waiting for transfers between devices: 119 us -> 61 us  [body(): lax.all_gather(tokens, both, axis=0, tiled=True)]
    all_gather x1 -> x0, waiting for transfers between devices: 41.3 us -> none  [body(): lax.all_gather(local, both, axis=0, tiled=True)]
    pallas_call x8 -> x4, Pallas kernels: 373 us -> 352 us  [the longest x1 166 us: expert_grads(): pl.pallas_call(functools.partial(grad_body, n_chunk), grid=(n_e, n_chunk...]
    pallas_call x2 -> x1, Pallas kernels: 37.3 us -> 33.1 us  [own_back(): pl.pallas_call(own_back_body, grid_spec=pltpu.PrefetchScalarGridSpec(num_...]
  transfers between devices with their start and end apart: 5 -> 4, of which waited for: 2 -> 1; matrix products, arithmetic and copies ran while one was open for 5% -> 5% of each run, Pallas kernels for 68% -> 71%
where the time goes in v2:
time: 634 us; the launch traced here: 632 us
  Pallas kernels  449 us (71%)
  blocking collectives  68.8 us (11%)
  waiting for transfers between devices  62.6 us (10%)
  other arithmetic  20.6 us (3%)
  local copies, waits for them, and re-layouts  16.4 us (3%)
  between operations  13.9 us (2%)
    pallas_call x1, Pallas kernels, expert_grads(): pl.pallas_call(functools.partial(grad_body, n_chunk), grid=(n_e, n_chunk...  166 us
    pallas_call x2, Pallas kernels, gather_rows(): pl.pallas_call(functools.partial(gather_body, caps, gate is not None, n_s...  99.6 us
    pallas_call x1, Pallas kernels, expert_in(): pl.pallas_call(functools.partial(fwd_body, n_chunk), grid_spec=pltpu.Pref...  86.4 us
    pallas_call x2, Pallas kernels, combine(): pl.pallas_call(functools.partial(combine_body, caps, gate is not None), g...  63.9 us
    all_gather x1, waiting for transfers between devices, body(): lax.all_gather(tokens, both, axis=0, tiled=True)  61 us
    all_gather x1, blocking collectives, body(): lax.all_gather(gates.T, both, axis=0, tiled=True)  34.4 us
    all_gather x1, blocking collectives, body(): lax.all_gather(routes.T, both, axis=0, tiled=True)  34.4 us
    pallas_call x1, Pallas kernels, own_back(): pl.pallas_call(own_back_body, grid_spec=pltpu.PrefetchScalarGridSpec(num_...  33.1 us
  transfers between devices with their start and end apart: 4, of which 1 were waited for; matrix products, arithmetic and copies ran while one was open for 5% of the time, Pallas kernels for 71%

profile of v2, /device:TPU:97, one launch (start us, length us, event | category | flops | bytes accessed | tf_op | source)
XLA Modules:
  0.0 632.2 jit_solution(10991042996668411239)
XLA Ops:
  7.2 0.0 copy-start.1
  7.2 0.1 all-gather.3.cloned.1.call-start
  7.3 0.7 all-gather.3.cloned.1.call-update
  8.0 0.1 all-gather.5.cloned.1.call-start
  8.1 0.7 all-gather.5.cloned.1.call-update
  8.8 0.1 reduce-scatter.3.cloned.1.call-start
  8.9 0.0 copy-done.1
  8.9 34.4 %all_gather.12 = s32[256,512]{1,0:T(8,128)S(1)} all-gather(s32[8,512]{1,0:T(8,128)S(1)} %bitcast.34), channel_id=1, replica_groups=mesh['pod'=1,'data'=4,'expert'=8] {'data','expert'}, dimensions={0}, use_global_device_ids=true | all-gather | bytes 540672 | tf_op jit(solution)/shard_map/all_gather | solution.py:316
  43.3 1.0 compare_reduce_fusion
  44.3 3.7 copy.20
  48.0 0.3 fusion.3
  48.3 0.0 copy-start.2
  48.3 4.7 copy.19
  53.0 0.0 copy-done.2
  53.0 34.4 %all_gather.13 = f32[256,512]{1,0:T(8,128)S(1)} all-gather(f32[8,512]{1,0:T(8,128)S(1)} %bitcast.35), channel_id=1, replica_groups=mesh['pod'=1,'data'=4,'expert'=8] {'data','expert'}, dimensions={0}, use_global_device_ids=true | all-gather | bytes 540672 | tf_op jit(solution)/shard_map/all_gather | solution.py:317
  87.4 1.0 fusion.1.refs_0_
  88.4 0.0 copy-start
  88.5 2.0 copy.24
  90.5 9.0 %convert_select_fusion = s32[32,5,512]{1,2,0:T(8,128)} fusion(f32[32,5,512]{1,2,0:T(8,128)} %copy.19, pred[32,5,512]{1,2,0:T(8,128)(4,1)S(1)} %copy.20, s32[5]{0:T(128)S(1)} %or_select_fusion), kind=kLoop, calls=%fused_computation | loop fusion | flops 327680 | bytes 737300 | tf_op jit(solution)/shard_map/jit(_where)/select_n | solution.py:327
  99.4 0.0 copy-done
  99.4 0.0 copy-start.3
  99.4 6.0 copy.22.rank_ref
  105.4 0.0 copy-done.3
  105.4 3.1 select_bitcast_fusion.slot_ref
  108.6 61.0 %all-gather.3.cloned.1.call-done = bf16[16384,1536]{1,0:T(8,128)(2,1)} async-done(((bf16[512,1536]{1,0:T(8,128)(2,1)}), bf16[16384,1536]{1,0:T(8,128)(2,1)}) %all-gather.3.cloned.1.call-update) | async-done | bytes 50331664 | tf_op jit(solution)/shard_map/all_gather | solution.py:318
  169.6 49.1 %gather_x.1 = bf16[6,32,104,1536]{3,2,1,0:T(8,128)(2,1)} custom-call(s32[32,5,512]{2,1,0:T(8,128)} %copy.22.rank_ref, bf16[32,512,1536]{2,1,0:T(8,128)(2,1)} %bitcast.37), custom_call_target="tpu_custom_call" | custom-call | flops 31406948352 | bytes 111673344 | tf_op jit(solution)/shard_map/gather_x/pallas_call | solution.py:97
  218.8 86.4 %expert_in.1 = (bf16[6,3328,512]{2,1,0:T(8,128)(2,1)}, bf16[6,3328,512]{2,1,0:T(8,128)(2,1)}, bf16[6,832,1536]{2,1,0:T(8,128)(2,1)}) custom-call(s32[1]{0:T(128)} %bitcast.7.q_ref, bf16[6,3328,1536]{2,1,0:T(8,128)(2,1)} %bitcast.38, bf16[5,1536,512]{2,1,0:T(8,128)(2,1)} %w1_ref.3, bf16[5,1536,512]{2,1,0:T(8,128)(2,1)} %w3_ref.3, bf16[5,512,1536]{2,1,0:T(8,128)(2,1)} %w2_ref.5), custom_call_target="tpu_custom_call" | custom-call | flops 62813896704 | bytes 102236160 | tf_op jit(solution)/shard_map/expert_in/pallas_call | solution.py:144
  305.2 42.5 %combine_y.1 = f32[4096,1536]{1,0:T(8,128)} custom-call(s32[8,512,5]{2,1,0:T(8,128)} %select_bitcast_fusion.slot_ref, f32[8,512,5]{2,1,0:T(8,128)} %bitcast.30, bf16[6,8,104,1536]{3,2,1,0:T(8,128)(2,1)} %bitcast.22, bf16[6,8,104,1536]{3,2,1,0:T(8,128)(2,1)} %bitcast.23, bf16[6,8,104,1536]{3,2,1,0:T(8,128)(2,1)} %bitcast.24, ...), custom_call_target="tpu_custom_call" | custom-call | flops 23555211264 | bytes 40501248 | tf_op jit(solution)/shard_map/combine_y/pallas_call | solution.py:225
  347.6 0.1 reduce-scatter.3.cloned.1.call-update
  347.7 0.1 reduce-scatter.5.cloned.1.call-start
  347.8 0.0 all-gather.5.cloned.1.call-done
  347.8 50.4 %gather_do.1 = bf16[6,32,104,1536]{3,2,1,0:T(8,128)(2,1)} custom-call(s32[32,5,512]{2,1,0:T(8,128)} %copy.22.rank_ref, f32[32,5,512]{2,1,0:T(8,128)} %copy-done, bf16[32,512,1536]{2,1,0:T(8,128)(2,1)} %bitcast.36), custom_call_target="tpu_custom_call" | custom-call | flops 31406948352 | bytes 111673344 | tf_op jit(solution)/shard_map/gather_do/pallas_call | solution.py:97
  398.3 33.1 %own_back.1 = bf16[6,832,1536]{2,1,0:T(8,128)(2,1)} custom-call(s32[1]{0:T(128)} %bitcast.7.q_ref, bf16[6,3328,1536]{2,1,0:T(8,128)(2,1)} %bitcast.27, bf16[6,3328,512]{2,1,0:T(8,128)(2,1)} %get-tuple-element.12.a_ref, bf16[6,3328,512]{2,1,0:T(8,128)(2,1)} %get-tuple-element.13.b_ref, bf16[5,1536,512]{2,1,0:T(8,128)(2,1)} %w1_ref.3, ...), custom_call_target="tpu_custom_call" | custom-call | flops 23555211264 | bytes 40894464 | tf_op jit(solution)/shard_map/own_back/pallas_call | solution.py:178
  431.3 21.4 %combine_dx.1 = f32[4096,1536]{1,0:T(8,128)} custom-call(s32[8,512,5]{2,1,0:T(8,128)} %select_bitcast_fusion.slot_ref, bf16[6,8,104,1536]{3,2,1,0:T(8,128)(2,1)} %bitcast.17, bf16[6,8,104,1536]{3,2,1,0:T(8,128)(2,1)} %bitcast.18, bf16[6,8,104,1536]{3,2,1,0:T(8,128)(2,1)} %bitcast.19, bf16[6,8,104,1536]{3,2,1,0:T(8,128)(2,1)} %bitcast.20, ...), custom_call_target="tpu_custom_call" | custom-call | flops 7851737088 | bytes 40501248 | tf_op jit(solution)/shard_map/combine_dx/pallas_call | solution.py:225
  452.8 0.1 reduce-scatter.5.cloned.1.call-update
  452.8 166.4 %expert_grads.1 = (f32[5,1536,512]{2,1,0:T(8,128)}, f32[5,1536,512]{2,1,0:T(8,128)}, f32[5,512,1536]{2,1,0:T(8,128)}) custom-call(bf16[6,3328,1536]{2,1,0:T(8,128)(2,1)} %bitcast.28, bf16[6,3328,512]{2,1,0:T(8,128)(2,1)} %get-tuple-element.12.a_ref, bf16[6,3328,512]{2,1,0:T(8,128)(2,1)} %get-tuple-element.13.b_ref, bf16[5,512,1536]{2,1,0:T(8,128)(2,1)} %w2_ref.5, ...), custom_call_target="tpu_custom_call" | custom-call | flops 125627793408 | bytes 224919552 | tf_op jit(solution)/shard_map/expert_grads/pallas_call | solution.py:281
  619.2 0.0 reduce-scatter.3.cloned.1.call-done
  619.2 3.2 convert_element_type.12
  622.5 0.0 reduce-scatter.5.cloned.1.call-done
  622.5 3.2 convert_element_type.13
  (3 shorter events, 0.0 us)
Async XLA Ops:
  7.2 1.7 copy-start.1
  7.2 162.4 %all-gather.3.cloned.1.call-start = ((), (), s32[]{:S(2)}) async-start(), calls=%async_computation.2 | async-start | bytes 51904512 | tf_op jit(solution)/shard_map/all_gather | solution.py:318
  8.0 339.8 %all-gather.5.cloned.1.call-start = ((), (), s32[]{:S(2)}) async-start(), calls=%async_computation.4 | async-start | bytes 51904512 | tf_op jit(solution)/shard_map/all_gather | solution.py:319
  8.8 610.4 %reduce-scatter.3.cloned.1.call-start = ((), (), s32[]{:S(2)}) async-start(), calls=%async_computation.3 | async-start | bytes 28311552 | tf_op jit(solution)/shard_map/reduce_scatter | solution.py:337
  48.3 4.7 copy-start.2
  88.4 11.0 %copy-start = (f32[32,5,512]{2,1,0:T(8,128)}, f32[32,5,512]{2,1,0:T(8,128)S(1)}, u32[]{:S(2)}) copy-start(f32[32,5,512]{2,1,0:T(8,128)S(1)} %fusion.1.refs_0_) | copy-start | bytes 983044
  99.4 6.0 copy-start.3
  347.7 274.8 %reduce-scatter.5.cloned.1.call-start = ((), (), s32[]{:S(2)}) async-start(), calls=%async_computation.5 | async-start | bytes 28311552 | tf_op jit(solution)/shard_map/reduce_scatter | solution.py:342
Sparse Core Ops, SparseCore 0:
  10.1 159.4 all-gather.2
  171.7 151.2 all-gather.4
  347.8 127.1 reduce-scatter.2
  477.2 128.5 reduce-scatter.4
